TPU v7x, 8 devices: a whole 2x2x1 slice. The times are simulated.
8 devices in a mesh: dp: 1 (over z), cz: 2 (over y), cy: 2 (over x), cx: 2 (over core).
Axes of the slice: x: 2, y: 2, z: 1, core: 2. Of those that a mesh axis runs over, the one named last changes fastest.
Arguments:
- x_tokens: bfloat16 [4096, 8192], P(('dp', 'cx', 'cz'), 'cy')
- w_up: bfloat16 [8192, 28672], P('cy', ('cz', 'cx'))
- w_down: bfloat16 [28672, 8192], P('cz', ('cy', 'cx'))
Outputs:
- output: bfloat16 [4096, 8192], P(('dp', 'cx', 'cz'), 'cy')
All inputs are finite; a program needn't handle non-finite values.
Results may differ from a plain program's by a relative error of at most 0.0114981.
Values are sent between devices in bfloat16 or wider.
A program may use at most 1 GiB of HBM per device.

v0:
```python
import jax
import jax.numpy as jnp
from jax import lax
from jax.sharding import PartitionSpec as P, NamedSharding


def solution(mesh):
    data_spec = P(('dp', 'cx', 'cz'), 'cy')
    up_spec = P('cy', ('cz', 'cx'))
    down_spec = P('cz', ('cy', 'cx'))

    def local_mlp(x_local, w_up_local, w_down_local):
        x_block = lax.all_gather(x_local, 'cz', axis=0, tiled=True)
        w_up_block = lax.all_gather(w_up_local, 'cx', axis=1, tiled=True)
        partial_up = jnp.dot(x_block, w_up_block, preferred_element_type=jnp.float32)
        pre_act = lax.psum_scatter(partial_up, 'cy', scatter_dimension=0, tiled=True)
        hidden = jax.nn.gelu(pre_act.astype(jnp.bfloat16).astype(jnp.float32), approximate=True).astype(jnp.bfloat16)
        hidden_block = lax.all_gather(hidden, 'cy', axis=0, tiled=True)
        w_down_block = lax.all_gather(w_down_local, 'cx', axis=1, tiled=True)
        partial_down = jnp.dot(hidden_block, w_down_block, preferred_element_type=jnp.float32)
        out_local = lax.psum_scatter(partial_down, 'cz', scatter_dimension=0, tiled=True)
        return out_local.astype(jnp.bfloat16)

    return jax.shard_map(local_mlp, mesh=mesh, in_specs=(data_spec, up_spec, down_spec), out_specs=data_spec, check_vma=False)
```

profile of v0, /device:TPU:0, one launch (start us, length us, event | category | flops | bytes accessed | tf_op | source)
XLA Modules:
  0.0 3360.9 jit_solution(11927200309178062100)
XLA Ops:
  6.5 0.0 all-gather.5.cloned.1.call-start
  6.5 0.7 all-gather.5.cloned.1.call-update
  7.3 0.0 all-gather.7.cloned.1.call-start
  7.3 0.7 all-gather.7.cloned.1.call-update
  8.0 0.0 reduce-scatter.7.cloned.1.call-start
  8.1 200.3 %all-gather.5.cloned.1.call-done = bf16[2048,4096]{1,0:T(8,128)(2,1)} async-done(((bf16[1024,4096]{1,0:T(8,128)(2,1)}), bf16[2048,4096]{1,0:T(8,128)(2,1)}) %all-gather.5.cloned.1.call-update) | async-done | bytes 16777232 | tf_op jit(solution)/shard_map/all_gather | solution.py:13
  208.4 156.7 %all-gather.7.cloned.1.call-done = bf16[4096,14336]{1,0:T(8,128)(2,1)} async-done(((bf16[4096,7168]{1,0:T(8,128)(2,1)}), bf16[4096,14336]{1,0:T(8,128)(2,1)}) %all-gather.7.cloned.1.call-update) | async-done | bytes 117440528 | tf_op jit(solution)/shard_map/all_gather | solution.py:14
  365.1 258.4 %fusion.6 = f32[2048,14336]{1,0:T(8,128)} fusion(bf16[2048,4096]{1,0:T(8,128)(2,1)} %all-gather.5.cloned.1.call-done, bf16[4096,14336]{1,0:T(8,128)(2,1)} %all-gather.7.cloned.1.call-done), kind=kOutput, calls=%fused_computation.10 | convolution fusion | flops 240518168576 | bytes 251658240 | tf_op jit(solution)/shard_map/dot_general | solution.py:15
  623.4 0.0 reduce-scatter.7.cloned.1.call-update
  623.5 0.0 all-gather.11.cloned.1.call-start
  623.5 0.5 all-gather.11.cloned.1.call-update
  624.0 0.0 all-gather.9.cloned.1.call-start
  624.1 1266.0 %reduce-scatter.7.cloned.1.call-done = f32[1024,14336]{1,0:T(8,128)} async-done(((f32[2048,14336]{1,0:T(8,128)}), f32[1024,14336]{1,0:T(8,128)}) %reduce-scatter.7.cloned.1.call-update) | async-done | bytes 58720272
  1890.1 29.8 fusion.5
  1919.9 0.0 all-gather.9.cloned.1.call-update
  1919.9 0.0 reduce-scatter.5.cloned.1.call-start
  1920.0 124.9 %all-gather.11.cloned.1.call-done = bf16[14336,4096]{1,0:T(8,128)(2,1)} async-done(((bf16[14336,2048]{1,0:T(8,128)(2,1)}), bf16[14336,4096]{1,0:T(8,128)(2,1)}) %all-gather.11.cloned.1.call-update) | async-done | bytes 117440528 | tf_op jit(solution)/shard_map/all_gather | solution.py:19
  2044.9 671.3 %all-gather.9.cloned.1.call-done = bf16[2048,14336]{1,0:T(8,128)(2,1)} async-done(((bf16[1024,14336]{1,0:T(8,128)(2,1)}), bf16[2048,14336]{1,0:T(8,128)(2,1)}) %all-gather.9.cloned.1.call-update) | async-done | bytes 58720272 | tf_op jit(solution)/shard_map/all_gather | solution.py:18
  2716.2 262.5 %fusion.7 = f32[2048,4096]{1,0:T(8,128)} fusion(bf16[2048,14336]{1,0:T(8,128)(2,1)} %all-gather.9.cloned.1.call-done, bf16[14336,4096]{1,0:T(8,128)(2,1)} %all-gather.11.cloned.1.call-done), kind=kOutput, calls=%fused_computation.11 | convolution fusion | flops 240518168576 | bytes 209715200 | tf_op jit(solution)/shard_map/dot_general | solution.py:20
  2978.8 0.0 reduce-scatter.5.cloned.1.call-update
  2978.8 366.3 %reduce-scatter.5.cloned.1.call-done = f32[1024,4096]{1,0:T(8,128)} async-done(((f32[2048,4096]{1,0:T(8,128)}), f32[1024,4096]{1,0:T(8,128)}) %reduce-scatter.5.cloned.1.call-update) | async-done | bytes 16777232 | tf_op jit(solution)/shard_map/reduce_scatter | solution.py:21
  3345.1 9.0 convert_element_type.15
Async XLA Ops:
  6.5 201.9 %all-gather.5.cloned.1.call-start = ((), (), s32[]{:S(2)}) async-start(), calls=%async_computation.2 | async-start | bytes 25165824 | tf_op jit(solution)/shard_map/all_gather | solution.py:13
  7.3 357.8 %all-gather.7.cloned.1.call-start = ((), (), s32[]{:S(2)}) async-start(), calls=%async_computation.3 | async-start | bytes 176160768 | tf_op jit(solution)/shard_map/all_gather | solution.py:14
  8.0 1882.1 %reduce-scatter.7.cloned.1.call-start = ((), (), s32[]{:S(2)}) async-start(), calls=%async_computation.7 | async-start | bytes 176160768
  623.5 1421.5 %all-gather.11.cloned.1.call-start = ((), (), s32[]{:S(2)}) async-start(), calls=%async_computation.5 | async-start | bytes 176160768 | tf_op jit(solution)/shard_map/all_gather | solution.py:19
  624.0 2092.2 %all-gather.9.cloned.1.call-start = ((), (), s32[]{:S(2)}) async-start(), calls=%async_computation.4 | async-start | bytes 88080384 | tf_op jit(solution)/shard_map/all_gather | solution.py:18
  1919.9 1425.1 %reduce-scatter.5.cloned.1.call-start = ((), (), s32[]{:S(2)}) async-start(), calls=%async_computation.6 | async-start | bytes 50331648 | tf_op jit(solution)/shard_map/reduce_scatter | solution.py:21
Sparse Core Ops, SparseCore 0:
  8.8 199.5 all-gather.4
  209.9 155.1 all-gather.6
  623.6 1266.5 reduce-scatter.6
  1891.5 153.3 all-gather.10
  2046.3 669.9 all-gather.8
  2978.9 366.0 reduce-scatter.4
where the time goes:
time: 3360 us
  waiting for transfers between devices  2790 us (83%)
  matrix products  521 us (16%)
  other arithmetic  38.8 us (1%)
    unnamed x7, waiting for transfers between devices  1270 us
    all_gather x1, waiting for transfers between devices, local_mlp(): hidden_block = lax.all_gather(hidden, 'cy', axis=0, tiled=True)  671 us
    reduce_scatter x1, waiting for transfers between devices, local_mlp(): lax.psum_scatter(partial_down, 'cz', scatter_dimension=0, tiled=True)  366 us
    dot_general x1, matrix products, local_mlp(): jnp.dot(hidden_block, w_down_block, preferred_element_type=jnp.float32)  263 us
    dot_general x1, matrix products, local_mlp(): jnp.dot(x_block, w_up_block, preferred_element_type=jnp.float32)  258 us
    all_gather x1, waiting for transfers between devices, local_mlp(): x_block = lax.all_gather(x_local, 'cz', axis=0, tiled=True)  200 us
    all_gather x1, waiting for transfers between devices, local_mlp(): w_up_block = lax.all_gather(w_up_local, 'cx', axis=1, tiled=True)  157 us
    all_gather x1, waiting for transfers between devices, local_mlp(): w_down_block = lax.all_gather(w_down_local, 'cx', axis=1, tiled=True)  125 us
  transfers between devices with their start and end apart: 6, of which 6 were waited for; matrix products, arithmetic and copies ran while one was open for 1% of the time, Pallas kernels for 0%

commit v1 on v0

v1 whole, which is shorter than its diff:
```python
import jax
import jax.numpy as jnp
from jax import lax
from jax.sharding import PartitionSpec as P


CHUNKS = (2, 2, 2, 1)
B_BLOCKS = (2, 2)
A_BLOCKS = (2, 1, 1)


def solution(mesh):
    data_spec = P(('dp', 'cx', 'cz'), 'cy')
    up_spec = P('cy', ('cz', 'cx'))
    down_spec = P('cz', ('cy', 'cx'))
    swap = [(0, 1), (1, 0)]

    def to_core(v):
        return lax.ppermute(v, 'cx', swap)

    def to_y(v):
        return lax.ppermute(v, 'cz', swap)

    def to_x(v):
        return lax.ppermute(v, 'cy', swap)

    def to_diag(v):
        return lax.ppermute(v, ('cy', 'cx'), [(0, 3), (1, 2), (2, 1), (3, 0)])

    def after(v, *deps):
        return lax.optimization_barrier((v, *deps))[0]

    def cat(pieces, axis):
        return pieces[0] if len(pieces) == 1 else jnp.concatenate(pieces, axis)

    def dot(a, b):
        return jnp.dot(a, b, preferred_element_type=jnp.float32)

    def gelu(c):
        c = lax.reduce_precision(c, 8, 7)
        return jax.nn.gelu(c, approximate=True).astype(jnp.bfloat16)

    def local_mlp(x, w1, w2):
        cy, cx = lax.axis_index('cy'), lax.axis_index('cx')
        rows, depth = x.shape
        half = w1.shape[1] // 2
        unit = half // sum(CHUNKS)
        starts = [unit * sum(CHUNKS[:j]) for j in range(len(CHUNKS))]
        sizes = [unit * c for c in CHUNKS]

        def columns(side, j):
            return lax.dynamic_slice(w1, (0, side * half + starts[j]), (depth, sizes[j]))

        x_o = to_x(x)
        w1_recv = []
        for j in range(len(CHUNKS)):
            piece = columns(1 - cy, j)
            if j:
                piece = after(piece, x_o if j == 1 else w1_recv[j - 2])
            w1_recv.append(to_x(piece))

        x_y = to_y(x)
        xo_y = to_y(x_o)

        def both(v):
            return after(jnp.concatenate([v, to_core(v)], 0))

        rows_own = {'A': both(x), 'B': both(x_y)}
        rows_oth = {'A': both(x_o), 'B': both(xo_y)}

        part_up = {'A': [], 'B': []}
        for name in 'AB':
            for j in range(len(CHUNKS)):
                part_up[name].append(after(dot(rows_own[name], columns(cy, j))))
        hid = {'A': [], 'B': []}
        for j in range(len(CHUNKS)):
            for name in 'BA':
                c = dot(rows_oth[name], w1_recv[j]) + part_up[name][j]
                hid[name].append(gelu(c))

        w2_o = to_core(w2)

        def down(quarters):
            width = w2.shape[1]
            buf = jnp.zeros((2 * half, 2 * width), w2.dtype)
            for r, (pcx, pcy) in enumerate(quarters):
                for c, w in enumerate((w2, w2_o)):
                    piece = lax.dynamic_slice(w, (pcx * (2 * half) + pcy * half, 0), (half, width))
                    buf = lax.dynamic_update_slice(buf, piece, (r * half, c * width))
            return after(buf)

        w2_own = down(((cx, cy), (1 - cx, cy)))
        w2_recv = down(((cx, 1 - cy), (1 - cx, 1 - cy)))

        blocks = []
        for name, shares in (('B', B_BLOCKS), ('A', A_BLOCKS)):
            step = rows // sum(shares)
            blocks += [(name, step * sum(shares[:k]), step * s) for k, s in enumerate(shares)]

        h_own, h_recv, arrived = [], [], []
        for i, (name, start, size) in enumerate(blocks):
            def part(chunks, base):
                return cat([hid[name][j][base + start:base + start + size] for j in chunks], 1)

            every = list(range(len(CHUNKS)))
            groups = [every[:-1], every[-1:]] if i == 0 else [every]
            own, core, xs, ds = [], [], [], []
            for chunks in groups:
                mine, theirs = part(chunks, 0), part(chunks, rows)
                if i >= 2:
                    mine, theirs = after((mine, theirs), arrived[i - 2])
                xs.append(to_x(mine))
                ds.append(to_diag(theirs))
                core.append(to_core(theirs))
                own.append(mine)
            arrived.append((xs[-1], ds[-1]))
            h_own.append(after(jnp.concatenate([*own, *core], 1)))
            h_recv.append(after(jnp.concatenate([*xs, *ds], 1)))

        from_y = []
        out = jnp.zeros(x.shape, x.dtype)
        for i, (name, start, size) in enumerate(blocks):
            z_own = after(dot(h_own[i], w2_own))
            if name == 'B':
                z = dot(h_recv[i], w2_recv) + z_own
                from_y.append((start, to_y(z)))
            else:
                base, rest = next((b, v) for b, v in reversed(from_y) if b <= start)
                z = (dot(h_recv[i], w2_recv) + z_own) + rest[start - base:start - base + size]
                z = z.astype(x.dtype)
                z = jnp.where(cx == 0, z, jnp.roll(z, depth // 2, 1))
                out = lax.dynamic_update_slice(out, z, (start, 0))
        return out

    return jax.shard_map(local_mlp, mesh=mesh, in_specs=(data_spec, up_spec, down_spec), out_specs=data_spec, check_vma=False)
```

time: 3360 us -> 2260 us (0.67)
  waiting for transfers between devices: 2790 us -> 1110 us
  local copies, waits for them, and re-layouts: 0 us -> 274 us
  matrix products: 521 us -> 698 us
  other arithmetic: 38.8 us -> 136 us
    unnamed x7 -> x0, waiting for transfers between devices: 1270 us -> none
    all_gather x4 -> x0, waiting for transfers between devices: 1150 us -> none  [the longest x1 671 us: local_mlp(): hidden_block = lax.all_gather(hidden, 'cy', axis=0, tiled=True)]
    ppermute x0 -> x32, waiting for transfers between devices: none -> 1110 us  [the longest x11 740 us: to_x(): return lax.ppermute(v, 'cy', swap)]
    reduce_scatter x1 -> x0, waiting for transfers between devices: 366 us -> none  [local_mlp(): lax.psum_scatter(partial_down, 'cz', scatter_dimension=0, tiled=True)]
    dot_general x2 -> x26, matrix products: 521 us -> 698 us  [dot(): return jnp.dot(a, b, preferred_element_type=jnp.float32)]
    dynamic_update_slice x0 -> x6, local copies, waits for them, and re-layouts: none -> 117 us  [the longest x5 112 us: down(): buf = lax.dynamic_update_slice(buf, piece, (r * half, c * width))]
    concatenate x0 -> x19, other arithmetic: none -> 100 us  [the longest x4 44.9 us: both(): return after(jnp.concatenate([v, to_core(v)], 0))]
    optimization_barrier x0 -> x8, local copies, waits for them, and re-layouts: none -> 65.8 us  [after(): return lax.optimization_barrier((v, *deps))[0]]
  transfers between devices with their start and end apart: 6 -> 32, of which waited for: 6 -> 15; matrix products, arithmetic and copies ran while one was open for 1% -> 41% of each run, Pallas kernels for 0% -> 0%
where the time goes in v1:
time: 2260 us; the launch traced here: 2250 us
  waiting for transfers between devices  1110 us (49%)
  matrix products  698 us (31%)
  local copies, waits for them, and re-layouts  274 us (12%)
  other arithmetic  136 us (6%)
  starting transfers between devices  26.3 us (1%)
    ppermute x11, waiting for transfers between devices, to_x(): return lax.ppermute(v, 'cy', swap)  740 us
    dot_general x26, matrix products, dot(): return jnp.dot(a, b, preferred_element_type=jnp.float32)  698 us
    ppermute x6, waiting for transfers between devices, to_diag(): return lax.ppermute(v, ('cy', 'cx'), [(0, 3), (1, 2), (2, 1), (3, 0)])  279 us
    dynamic_update_slice x5, local copies, waits for them, and re-layouts, down(): buf = lax.dynamic_update_slice(buf, piece, (r * half, c * width))  112 us
    ppermute x4, waiting for transfers between devices, to_y(): return lax.ppermute(v, 'cz', swap)  96.4 us
    optimization_barrier x8, local copies, waits for them, and re-layouts, after(): return lax.optimization_barrier((v, *deps))[0]  65.8 us
  transfers between devices with their start and end apart: 32, of which 15 were waited for; matrix products, arithmetic and copies ran while one was open for 41% of the time, Pallas kernels for 0%

profile of v1, /device:TPU:0, one launch (start us, length us, event | category | flops | bytes accessed | tf_op | source)
XLA Modules:
  0.0 2249.0 jit_solution(9020748494604798270)
XLA Ops:
  94.4 107.5 %collective-permute-done.2 = bf16[4096,1024]{1,0:T(8,128)(2,1)} collective-permute-done((bf16[4096,1024]{1,0:T(8,128)(2,1)}, bf16[4096,1024]{1,0:T(8,128)(2,1)}, u32[]{:S(2)}, u32[]{:S(2)}) %collective-permute-start.2) | collective-permute-done | bytes 8388640 | tf_op jit(solution)/shard_map/ppermute | solution.py:25
  249.5 132.2 %collective-permute-done = bf16[1024,4096]{1,0:T(8,128)(2,1)} collective-permute-done((bf16[1024,4096]{1,0:T(8,128)(2,1)}, bf16[1024,4096]{1,0:T(8,128)(2,1)}, u32[]{:S(2)}, u32[]{:S(2)}) %collective-permute-start) | collective-permute-done | bytes 8388640 | tf_op jit(solution)/shard_map/ppermute | solution.py:25
  404.5 24.5 %fusion.54 = f32[2048,1024]{1,0:T(8,128)} fusion(bf16[2048,4096]{1,0:T(8,128)(2,1)} %copy-done.4, bf16[4096,7168]{1,0:T(8,128)(2,1)} %param.4, s32[]{:T(128)S(6)} %select_n.68), kind=kOutput, calls=%fused_computation.71 | convolution fusion | flops 17179869184 | bytes 33554436 | tf_op jit(solution)/shard_map/dot_general | solution.py:37
  486.4 253.9 %collective-permute-done.4 = bf16[4096,1024]{1,0:T(8,128)(2,1)} collective-permute-done((bf16[4096,1024]{1,0:T(8,128)(2,1)}, bf16[4096,1024]{1,0:T(8,128)(2,1)}, u32[]{:S(2)}, u32[]{:S(2)}) %collective-permute-start.4) | collective-permute-done | bytes 8388640 | tf_op jit(solution)/shard_map/ppermute | solution.py:25
  787.8 24.0 %fusion.52 = f32[2048,1024]{1,0:T(8,128)} fusion(bf16[2048,4096]{1,0:T(8,128)(2,1)} %copy-done.5, bf16[4096,7168]{1,0:T(8,128)(2,1)} %param.4, s32[]{:T(128)S(6)} %select_n.68), kind=kOutput, calls=%fused_computation.69 | convolution fusion | flops 17179869184 | bytes 33554436 | tf_op jit(solution)/shard_map/dot_general | solution.py:37
  874.5 25.7 %fusion.23 = bf16[2048,1024]{0,1:T(8,128)(2,1)S(1)} fusion(f32[2048,1024]{0,1:T(8,128)} %copy.6, bf16[2048,4096]{1,0:T(8,128)(2,1)} %pad_maximum_fusion, bf16[4096,1024]{1,0:T(8,128)(2,1)} %collective-permute-done.5), kind=kOutput, calls=%fused_computation.39 | convolution fusion | flops 17202937856 | bytes 37748736 | tf_op jit(solution)/shard_map/dot_general | solution.py:37
  901.7 27.0 %fusion.15 = bf16[2048,1024]{0,1:T(8,128)(2,1)} fusion(f32[2048,1024]{0,1:T(8,128)} %copy.5, bf16[2048,4096]{1,0:T(8,128)(2,1)} %pad_maximum_fusion, bf16[4096,1024]{1,0:T(8,128)(2,1)} %collective-permute-done.4), kind=kOutput, calls=%fused_computation.31 | convolution fusion | flops 17202937856 | bytes 37748736 | tf_op jit(solution)/shard_map/dot_general | solution.py:37
  931.7 26.7 %fusion.7 = bf16[2048,1024]{0,1:T(8,128)(2,1)} fusion(f32[2048,1024]{0,1:T(8,128)} %copy.4, bf16[2048,4096]{1,0:T(8,128)(2,1)} %pad_maximum_fusion, bf16[4096,1024]{1,0:T(8,128)(2,1)} %collective-permute-done.2), kind=kOutput, calls=%fused_computation.23 | convolution fusion | flops 17202937856 | bytes 37748736 | tf_op jit(solution)/shard_map/dot_general | solution.py:37
  980.2 24.4 %fusion.108 = f32[2048,1024]{0,1:T(8,128)} fusion(bf16[2048,4096]{1,0:T(8,128)(2,1)} %pad_maximum_fusion.2, bf16[4096,1024]{1,0:T(8,128)(2,1)} %collective-permute-done.2), kind=kOutput, calls=%fused_computation.169 | convolution fusion | flops 17179869184 | bytes 33554432 | tf_op jit(solution)/shard_map/dot_general | solution.py:37
  1012.9 24.4 %fusion.109 = f32[2048,1024]{0,1:T(8,128)} fusion(bf16[2048,4096]{1,0:T(8,128)(2,1)} %pad_maximum_fusion.2, bf16[4096,1024]{1,0:T(8,128)(2,1)} %collective-permute-done.4), kind=kOutput, calls=%fused_computation.170 | convolution fusion | flops 17179869184 | bytes 33554432 | tf_op jit(solution)/shard_map/dot_general | solution.py:37
  1046.4 24.3 %fusion.110 = f32[2048,1024]{0,1:T(8,128)} fusion(bf16[2048,4096]{1,0:T(8,128)(2,1)} %pad_maximum_fusion.2, bf16[4096,1024]{1,0:T(8,128)(2,1)} %collective-permute-done.5), kind=kOutput, calls=%fused_computation.171 | convolution fusion | flops 17179869184 | bytes 33554432 | tf_op jit(solution)/shard_map/dot_general | solution.py:37
  1108.6 54.2 %collective-permute-done.11 = bf16[512,512]{0,1:T(8,128)(2,1)S(1)} collective-permute-done((bf16[512,512]{0,1:T(8,128)(2,1)S(1)}, bf16[512,512]{0,1:T(8,128)(2,1)S(1)}, u32[]{:S(2)}, u32[]{:S(2)}) %collective-permute-start.11) | collective-permute-done | bytes 524320 | tf_op jit(solution)/shard_map/ppermute | solution.py:25
  1194.8 45.8 %collective-permute-done.18 = bf16[512,3072]{0,1:T(8,128)(2,1)} collective-permute-done((bf16[512,3072]{0,1:T(8,128)(2,1)}, bf16[512,3072]{0,1:T(8,128)(2,1)}, u32[]{:S(2)}, u32[]{:S(2)}) %collective-permute-start.18) | collective-permute-done | bytes 3145760 | tf_op jit(solution)/shard_map/ppermute | solution.py:28
  1248.8 71.4 %collective-permute-done.22 = bf16[512,3584]{0,1:T(8,128)(2,1)} collective-permute-done((bf16[512,3584]{0,1:T(8,128)(2,1)}, bf16[512,3584]{0,1:T(8,128)(2,1)}, u32[]{:S(2)}, u32[]{:S(2)}) %collective-permute-start.22) | collective-permute-done | bytes 3670048 | tf_op jit(solution)/shard_map/ppermute | solution.py:25
  1324.3 73.6 %collective-permute-done.23 = bf16[512,3584]{0,1:T(8,128)(2,1)} collective-permute-done((bf16[512,3584]{0,1:T(8,128)(2,1)}, bf16[512,3584]{0,1:T(8,128)(2,1)}, u32[]{:S(2)}, u32[]{:S(2)}) %collective-permute-start.23) | collective-permute-done | bytes 3670048 | tf_op jit(solution)/shard_map/ppermute | solution.py:28
  1420.8 56.7 %collective-permute-done.13 = bf16[512,3584]{0,1:T(8,128)(2,1)} collective-permute-done((bf16[512,3584]{0,1:T(8,128)(2,1)S(1)}, bf16[512,3584]{0,1:T(8,128)(2,1)}, u32[]{:S(2)}, u32[]{:S(2)}) %collective-permute-start.13) | collective-permute-done | bytes 3670048 | tf_op jit(solution)/shard_map/ppermute | solution.py:25
  1477.5 77.7 %collective-permute-done.14 = bf16[512,3584]{0,1:T(8,128)(2,1)} collective-permute-done((bf16[512,3584]{0,1:T(8,128)(2,1)}, bf16[512,3584]{0,1:T(8,128)(2,1)}, u32[]{:S(2)}, u32[]{:S(2)}) %collective-permute-start.14) | collective-permute-done | bytes 3670048 | tf_op jit(solution)/shard_map/ppermute | solution.py:28
  1562.9 32.5 %collective-permute-done.24 = bf16[256,3584]{0,1:T(8,128)(2,1)} collective-permute-done((bf16[256,3584]{0,1:T(8,128)(2,1)}, bf16[256,3584]{0,1:T(8,128)(2,1)}, u32[]{:S(2)}, u32[]{:S(2)}) %collective-permute-start.24) | collective-permute-done | bytes 1835040 | tf_op jit(solution)/shard_map/ppermute | solution.py:25
  1600.9 32.9 %collective-permute-done.25 = bf16[256,3584]{0,1:T(8,128)(2,1)} collective-permute-done((bf16[256,3584]{0,1:T(8,128)(2,1)}, bf16[256,3584]{0,1:T(8,128)(2,1)}, u32[]{:S(2)}, u32[]{:S(2)}) %collective-permute-start.25) | collective-permute-done | bytes 1835040 | tf_op jit(solution)/shard_map/ppermute | solution.py:28
  1643.0 31.1 %collective-permute-done.29 = bf16[256,3584]{0,1:T(8,128)(2,1)} collective-permute-done((bf16[256,3584]{0,1:T(8,128)(2,1)}, bf16[256,3584]{0,1:T(8,128)(2,1)}, u32[]{:S(2)}, u32[]{:S(2)}) %collective-permute-start.29) | collective-permute-done | bytes 1835040 | tf_op jit(solution)/shard_map/ppermute | solution.py:25
  1674.1 38.4 %collective-permute-done.30 = bf16[256,3584]{0,1:T(8,128)(2,1)} collective-permute-done((bf16[256,3584]{0,1:T(8,128)(2,1)}, bf16[256,3584]{0,1:T(8,128)(2,1)}, u32[]{:S(2)}, u32[]{:S(2)}) %collective-permute-start.30) | collective-permute-done | bytes 1835040 | tf_op jit(solution)/shard_map/ppermute | solution.py:28
  1785.5 39.6 %fusion.113 = f32[512,4096]{1,0:T(8,128)} fusion(bf16[512,7168]{0,1:T(8,128)(2,1)} %constant_dynamic-update-slice_fusion.6, bf16[7168,4096]{1,0:T(8,128)(2,1)} %get-tuple-element.24), kind=kOutput, calls=%fused_computation.174 | convolution fusion | flops 30064771072 | bytes 74448896 | tf_op jit(solution)/shard_map/dot_general | solution.py:37
  1825.1 40.4 %convolution_add_fusion = f32[512,4096]{1,0:T(8,128)} fusion(f32[512,4096]{1,0:T(8,128)} %fusion.113, bf16[512,7168]{0,1:T(8,128)(2,1)} %pad_maximum_fusion.7, bf16[7168,4096]{1,0:T(8,128)(2,1)} %get-tuple-element.23), kind=kOutput, calls=%fused_computation.83 | convolution fusion | flops 30066868224 | bytes 82837504 | tf_op jit(solution)/shard_map/dot_general | solution.py:37
  1867.0 39.6 %fusion.107 = f32[512,4096]{1,0:T(8,128)} fusion(bf16[512,7168]{0,1:T(8,128)(2,1)} %pad_maximum_fusion.5, bf16[7168,4096]{1,0:T(8,128)(2,1)} %get-tuple-element.24), kind=kOutput, calls=%fused_computation.168 | convolution fusion | flops 30064771072 | bytes 74448896 | tf_op jit(solution)/shard_map/dot_general | solution.py:37
  1906.6 40.0 %fusion.111 = f32[512,4096]{1,0:T(8,128)} fusion(bf16[512,7168]{0,1:T(8,128)(2,1)} %constant_dynamic-update-slice_fusion, bf16[7168,4096]{1,0:T(8,128)(2,1)} %get-tuple-element.24), kind=kOutput, calls=%fused_computation.172 | convolution fusion | flops 30064771072 | bytes 74448896 | tf_op jit(solution)/shard_map/dot_general | solution.py:37
  1946.6 40.4 %convolution_add_fusion.1 = f32[512,4096]{1,0:T(8,128)} fusion(f32[512,4096]{1,0:T(8,128)} %fusion.111, bf16[512,7168]{0,1:T(8,128)(2,1)} %pad_maximum_fusion.6, bf16[7168,4096]{1,0:T(8,128)(2,1)} %get-tuple-element.23), kind=kOutput, calls=%fused_computation.84 | convolution fusion | flops 30066868224 | bytes 82837504 | tf_op jit(solution)/shard_map/dot_general | solution.py:37
  1987.4 25.1 %fusion.114 = f32[256,4096]{1,0:T(8,128)} fusion(bf16[256,7168]{0,1:T(8,128)(2,1)S(1)} %copy-done.1, bf16[7168,4096]{1,0:T(8,128)(2,1)} %get-tuple-element.24), kind=kOutput, calls=%fused_computation.175 | convolution fusion | flops 15032385536 | bytes 66584576 | tf_op jit(solution)/shard_map/dot_general | solution.py:37
  2012.5 39.7 %fusion.106 = f32[512,4096]{1,0:T(8,128)} fusion(bf16[512,7168]{0,1:T(8,128)(2,1)} %pad_maximum_fusion.4, bf16[7168,4096]{1,0:T(8,128)(2,1)} %get-tuple-element.23), kind=kOutput, calls=%fused_computation.167 | convolution fusion | flops 30064771072 | bytes 74448896 | tf_op jit(solution)/shard_map/dot_general | solution.py:37
  2052.3 25.1 %fusion.112 = f32[256,4096]{1,0:T(8,128)} fusion(bf16[256,7168]{0,1:T(8,128)(2,1)S(1)} %copy-done, bf16[7168,4096]{1,0:T(8,128)(2,1)} %get-tuple-element.24), kind=kOutput, calls=%fused_computation.173 | convolution fusion | flops 15032385536 | bytes 66584576 | tf_op jit(solution)/shard_map/dot_general | solution.py:37
  2077.4 27.7 %fusion.62 = bf16[256,4096]{1,0:T(8,128)(2,1)S(1)} fusion(f32[256,4096]{1,0:T(8,128)} %fusion.114, bf16[256,7168]{0,1:T(8,128)(2,1)} %pad_maximum_fusion.14, bf16[7168,4096]{1,0:T(8,128)(2,1)} %get-tuple-element.23, f32[512,4096]{1,0:T(8,128)} %collective-permute-done.28), kind=kOutput, calls=%fused_computation.89 | convolution fusion | flops 15035531264 | bytes 72876032 | tf_op jit(solution)/shard_map/dot_general | solution.py:37
  2106.7 24.9 %fusion.63 = bf16[256,4096]{1,0:T(8,128)(2,1)S(1)} fusion(f32[256,4096]{1,0:T(8,128)S(1)} %copy-done.3, bf16[256,7168]{0,1:T(8,128)(2,1)S(1)} %copy-done.2, bf16[7168,4096]{1,0:T(8,128)(2,1)} %get-tuple-element.23, f32[512,4096]{1,0:T(8,128)} %collective-permute-done.28), kind=kOutput, calls=%fused_computation.90 | convolution fusion | flops 15035531264 | bytes 72876032 | tf_op jit(solution)/shard_map/dot_general | solution.py:37
  2131.9 96.4 %collective-permute-done.21 = f32[512,4096]{1,0:T(8,128)} collective-permute-done((f32[512,4096]{1,0:T(8,128)}, f32[512,4096]{1,0:T(8,128)}, u32[]{:S(2)}, u32[]{:S(2)}) %collective-permute-start.21) | collective-permute-done | bytes 8388640 | tf_op jit(solution)/shard_map/ppermute | solution.py:22
  (217 shorter events, 600.2 us)
Async XLA Ops:
  17.0 184.9 %collective-permute-start.2 = (bf16[4096,1024]{1,0:T(8,128)(2,1)}, bf16[4096,1024]{1,0:T(8,128)(2,1)}, u32[]{:S(2)}, u32[]{:S(2)}) collective-permute-start(bf16[4096,1024]{1,0:T(8,128)(2,1)} %get-tuple-element.33), channel_id=1, source_target_pairs={{0,2},{2,0},{1,3},{3,1},{4,6},{6,4},{5,7},{7,5}} | collective-permute-start | bytes 25165832 | tf_op jit(solution)/shard_map/ppermute | solution.py:25
  20.3 183.6 %collective-permute-start.3 = (bf16[1024,4096]{1,0:T(8,128)(2,1)}, bf16[1024,4096]{1,0:T(8,128)(2,1)}, u32[]{:S(2)}, u32[]{:S(2)}) collective-permute-start(bf16[1024,4096]{1,0:T(8,128)(2,1)} %param.3), channel_id=1, source_target_pairs={{0,1},{1,0},{2,3},{3,2},{4,5},{5,4},{6,7},{7,6}} | collective-permute-start | bytes 25165832 | tf_op jit(solution)/shard_map/ppermute | solution.py:19
  20.3 361.4 %collective-permute-start = (bf16[1024,4096]{1,0:T(8,128)(2,1)}, bf16[1024,4096]{1,0:T(8,128)(2,1)}, u32[]{:S(2)}, u32[]{:S(2)}) collective-permute-start(bf16[1024,4096]{1,0:T(8,128)(2,1)} %param.3), channel_id=1, source_target_pairs={{0,2},{2,0},{1,3},{3,1},{4,6},{6,4},{5,7},{7,5}} | collective-permute-start | bytes 25165832 | tf_op jit(solution)/shard_map/ppermute | solution.py:25
  20.3 383.6 %collective-permute-start.9 = (bf16[1024,4096]{1,0:T(8,128)(2,1)}, bf16[1024,4096]{1,0:T(8,128)(2,1)}, u32[]{:S(2)}, u32[]{:S(2)}) collective-permute-start(bf16[1024,4096]{1,0:T(8,128)(2,1)} %param.3), channel_id=1, source_target_pairs={{0,4},{4,0},{1,5},{5,1},{2,6},{6,2},{3,7},{7,3}} | collective-permute-start | bytes 25165832 | tf_op jit(solution)/shard_map/ppermute | solution.py:22
  22.4 1696.4 %collective-permute-start.15 = (bf16[14336,2048]{1,0:T(8,128)(2,1)}, bf16[14336,2048]{1,0:T(8,128)(2,1)}, u32[]{:S(2)}, u32[]{:S(2)}) collective-permute-start(bf16[14336,2048]{1,0:T(8,128)(2,1)} %param.5), channel_id=1, source_target_pairs={{0,1},{1,0},{2,3},{3,2},{4,5},{5,4},{6,7},{7,6}} | collective-permute-start | bytes 176160768 | tf_op jit(solution)/shard_map/ppermute | solution.py:19
  201.9 672.6 %collective-permute-start.5 = (bf16[4096,1024]{1,0:T(8,128)(2,1)}, bf16[4096,1024]{1,0:T(8,128)(2,1)}, u32[]{:S(2)}, u32[]{:S(2)}) collective-permute-start(bf16[4096,1024]{1,0:T(8,128)(2,1)} %get-tuple-element.15), channel_id=1, source_target_pairs={{0,2},{2,0},{1,3},{3,1},{4,6},{6,4},{5,7},{7,5}} | collective-permute-start | bytes 25165832 | tf_op jit(solution)/shard_map/ppermute | solution.py:25
  381.7 358.7 %collective-permute-start.4 = (bf16[4096,1024]{1,0:T(8,128)(2,1)}, bf16[4096,1024]{1,0:T(8,128)(2,1)}, u32[]{:S(2)}, u32[]{:S(2)}) collective-permute-start(bf16[4096,1024]{1,0:T(8,128)(2,1)} %get-tuple-element.14), channel_id=1, source_target_pairs={{0,2},{2,0},{1,3},{3,1},{4,6},{6,4},{5,7},{7,5}} | collective-permute-start | bytes 25165832 | tf_op jit(solution)/shard_map/ppermute | solution.py:25
  383.7 87.6 %collective-permute-start.1 = (bf16[1024,4096]{1,0:T(8,128)(2,1)}, bf16[1024,4096]{1,0:T(8,128)(2,1)}, u32[]{:S(2)}, u32[]{:S(2)}) collective-permute-start(bf16[1024,4096]{1,0:T(8,128)(2,1)} %collective-permute-done), channel_id=1, source_target_pairs={{0,1},{1,0},{2,3},{3,2},{4,5},{5,4},{6,7},{7,6}} | collective-permute-start | bytes 25165832 | tf_op jit(solution)/shard_map/ppermute | solution.py:19
  404.0 338.1 %collective-permute-start.10 = (bf16[1024,4096]{1,0:T(8,128)(2,1)}, bf16[1024,4096]{1,0:T(8,128)(2,1)}, u32[]{:S(2)}, u32[]{:S(2)}) collective-permute-start(bf16[1024,4096]{1,0:T(8,128)(2,1)} %collective-permute-done.9), channel_id=1, source_target_pairs={{0,1},{1,0},{2,3},{3,2},{4,5},{5,4},{6,7},{7,6}} | collective-permute-start | bytes 25165832 | tf_op jit(solution)/shard_map/ppermute | solution.py:19
  471.3 403.3 %collective-permute-start.7 = (bf16[1024,4096]{1,0:T(8,128)(2,1)}, bf16[1024,4096]{1,0:T(8,128)(2,1)}, u32[]{:S(2)}, u32[]{:S(2)}) collective-permute-start(bf16[1024,4096]{1,0:T(8,128)(2,1)} %collective-permute-done), channel_id=1, source_target_pairs={{0,4},{4,0},{1,5},{5,1},{2,6},{6,2},{3,7},{7,3}} | collective-permute-start | bytes 25165832 | tf_op jit(solution)/shard_map/ppermute | solution.py:22
  740.4 340.5 %collective-permute-start.6 = (bf16[4096,512]{1,0:T(8,128)(2,1)}, bf16[4096,512]{1,0:T(8,128)(2,1)}, u32[]{:S(2)}, u32[]{:S(2)}) collective-permute-start(bf16[4096,512]{1,0:T(8,128)(2,1)} %constant_dynamic-slice_fusion.2), channel_id=1, source_target_pairs={{0,2},{2,0},{1,3},{3,1},{4,6},{6,4},{5,7},{7,5}} | collective-permute-start | bytes 12582920 | tf_op jit(solution)/shard_map/ppermute | solution.py:25
  874.5 91.7 %collective-permute-start.8 = (bf16[1024,4096]{1,0:T(8,128)(2,1)}, bf16[1024,4096]{1,0:T(8,128)(2,1)}, u32[]{:S(2)}, u32[]{:S(2)}) collective-permute-start(bf16[1024,4096]{1,0:T(8,128)(2,1)} %collective-permute-done.7), channel_id=1, source_target_pairs={{0,1},{1,0},{2,3},{3,2},{4,5},{5,4},{6,7},{7,6}} | collective-permute-start | bytes 25165832 | tf_op jit(solution)/shard_map/ppermute | solution.py:19
  1080.4 96.1 %collective-permute-start.17 = (bf16[512,3072]{0,1:T(8,128)(2,1)}, bf16[512,3072]{0,1:T(8,128)(2,1)}, u32[]{:S(2)}, u32[]{:S(2)}) collective-permute-start(bf16[512,3072]{0,1:T(8,128)(2,1)} %pad_maximum_fusion.16), channel_id=1, source_target_pairs={{0,2},{2,0},{1,3},{3,1},{4,6},{6,4},{5,7},{7,5}} | collective-permute-start | bytes 9437192 | tf_op jit(solution)/shard_map/ppermute | solution.py:25
  1101.8 60.9 %collective-permute-start.11 = (bf16[512,512]{0,1:T(8,128)(2,1)S(1)}, bf16[512,512]{0,1:T(8,128)(2,1)S(1)}, u32[]{:S(2)}, u32[]{:S(2)}) collective-permute-start(bf16[512,512]{0,1:T(8,128)(2,1)S(1)} %get-tuple-element.85), channel_id=1, source_target_pairs={{0,2},{2,0},{1,3},{3,1},{4,6},{6,4},{5,7},{7,5}} | collective-permute-start | bytes 1572872 | tf_op jit(solution)/shard_map/ppermute | solution.py:25
  1103.0 70.0 %collective-permute-start.12 = (bf16[512,512]{0,1:T(8,128)(2,1)S(1)}, bf16[512,512]{0,1:T(8,128)(2,1)S(1)}, u32[]{:S(2)}, u32[]{:S(2)}) collective-permute-start(bf16[512,512]{0,1:T(8,128)(2,1)S(1)} %get-tuple-element.84), channel_id=1, source_target_pairs={{0,3},{1,2},{2,1},{3,0},{4,7},{5,6},{6,5},{7,4}} | collective-permute-start | bytes 1572872 | tf_op jit(solution)/shard_map/ppermute | solution.py:28
  1105.1 135.5 %collective-permute-start.18 = (bf16[512,3072]{0,1:T(8,128)(2,1)}, bf16[512,3072]{0,1:T(8,128)(2,1)}, u32[]{:S(2)}, u32[]{:S(2)}) collective-permute-start(bf16[512,3072]{0,1:T(8,128)(2,1)} %pad_maximum_fusion.17), channel_id=1, source_target_pairs={{0,3},{1,2},{2,1},{3,0},{4,7},{5,6},{6,5},{7,4}} | collective-permute-start | bytes 9437192 | tf_op jit(solution)/shard_map/ppermute | solution.py:28
  1162.8 12.8 collective-permute-start.20
  1173.1 147.1 %collective-permute-start.22 = (bf16[512,3584]{0,1:T(8,128)(2,1)}, bf16[512,3584]{0,1:T(8,128)(2,1)}, u32[]{:S(2)}, u32[]{:S(2)}) collective-permute-start(bf16[512,3584]{0,1:T(8,128)(2,1)} %pad_maximum_fusion.10), channel_id=1, source_target_pairs={{0,2},{2,0},{1,3},{3,1},{4,6},{6,4},{5,7},{7,5}} | collective-permute-start | bytes 11010056 | tf_op jit(solution)/shard_map/ppermute | solution.py:25
  1175.6 72.7 %collective-permute-start.19 = (bf16[512,3072]{0,1:T(8,128)(2,1)}, bf16[512,3072]{0,1:T(8,128)(2,1)}, u32[]{:S(2)}, u32[]{:S(2)}) collective-permute-start(bf16[512,3072]{0,1:T(8,128)(2,1)} %pad_maximum_fusion.17), channel_id=1, source_target_pairs={{0,1},{1,0},{2,3},{3,2},{4,5},{5,4},{6,7},{7,6}} | collective-permute-start | bytes 9437192 | tf_op jit(solution)/shard_map/ppermute | solution.py:19
  1176.4 221.4 %collective-permute-start.23 = (bf16[512,3584]{0,1:T(8,128)(2,1)}, bf16[512,3584]{0,1:T(8,128)(2,1)}, u32[]{:S(2)}, u32[]{:S(2)}) collective-permute-start(bf16[512,3584]{0,1:T(8,128)(2,1)} %pad_maximum_fusion.11), channel_id=1, source_target_pairs={{0,3},{1,2},{2,1},{3,0},{4,7},{5,6},{6,5},{7,4}} | collective-permute-start | bytes 11010056 | tf_op jit(solution)/shard_map/ppermute | solution.py:28
  1240.6 169.0 %collective-permute-start.27 = (bf16[512,3584]{0,1:T(8,128)(2,1)}, bf16[512,3584]{0,1:T(8,128)(2,1)}, u32[]{:S(2)}, u32[]{:S(2)}) collective-permute-start(bf16[512,3584]{0,1:T(8,128)(2,1)} %pad_maximum_fusion.11), channel_id=1, source_target_pairs={{0,1},{1,0},{2,3},{3,2},{4,5},{5,4},{6,7},{7,6}} | collective-permute-start | bytes 11010056 | tf_op jit(solution)/shard_map/ppermute | solution.py:19
  1248.3 229.2 %collective-permute-start.13 = (bf16[512,3584]{0,1:T(8,128)(2,1)S(1)}, bf16[512,3584]{0,1:T(8,128)(2,1)}, u32[]{:S(2)}, u32[]{:S(2)}) collective-permute-start(bf16[512,3584]{0,1:T(8,128)(2,1)S(1)} %get-tuple-element.17), channel_id=1, source_target_pairs={{0,2},{2,0},{1,3},{3,1},{4,6},{6,4},{5,7},{7,5}} | collective-permute-start | bytes 11010056 | tf_op jit(solution)/shard_map/ppermute | solution.py:25
  1320.2 235.0 %collective-permute-start.14 = (bf16[512,3584]{0,1:T(8,128)(2,1)}, bf16[512,3584]{0,1:T(8,128)(2,1)}, u32[]{:S(2)}, u32[]{:S(2)}) collective-permute-start(bf16[512,3584]{0,1:T(8,128)(2,1)} %get-tuple-element.18), channel_id=1, source_target_pairs={{0,3},{1,2},{2,1},{3,0},{4,7},{5,6},{6,5},{7,4}} | collective-permute-start | bytes 11010056 | tf_op jit(solution)/shard_map/ppermute | solution.py:28
  1397.9 164.6 %collective-permute-start.16 = (bf16[512,3584]{0,1:T(8,128)(2,1)}, bf16[512,3584]{0,1:T(8,128)(2,1)}, u32[]{:S(2)}, u32[]{:S(2)}) collective-permute-start(bf16[512,3584]{0,1:T(8,128)(2,1)} %get-tuple-element.18), channel_id=1, source_target_pairs={{0,1},{1,0},{2,3},{3,2},{4,5},{5,4},{6,7},{7,6}} | collective-permute-start | bytes 11010056 | tf_op jit(solution)/shard_map/ppermute | solution.py:19
  1409.6 185.9 %collective-permute-start.24 = (bf16[256,3584]{0,1:T(8,128)(2,1)}, bf16[256,3584]{0,1:T(8,128)(2,1)}, u32[]{:S(2)}, u32[]{:S(2)}) collective-permute-start(bf16[256,3584]{0,1:T(8,128)(2,1)} %get-tuple-element.19), channel_id=1, source_target_pairs={{0,2},{2,0},{1,3},{3,1},{4,6},{6,4},{5,7},{7,5}} | collective-permute-start | bytes 5505032 | tf_op jit(solution)/shard_map/ppermute | solution.py:25
  1477.5 156.3 %collective-permute-start.25 = (bf16[256,3584]{0,1:T(8,128)(2,1)}, bf16[256,3584]{0,1:T(8,128)(2,1)}, u32[]{:S(2)}, u32[]{:S(2)}) collective-permute-start(bf16[256,3584]{0,1:T(8,128)(2,1)} %get-tuple-element.20), channel_id=1, source_target_pairs={{0,3},{1,2},{2,1},{3,0},{4,7},{5,6},{6,5},{7,4}} | collective-permute-start | bytes 5505032 | tf_op jit(solution)/shard_map/ppermute | solution.py:28
  1555.2 83.6 %collective-permute-start.26 = (bf16[256,3584]{0,1:T(8,128)(2,1)}, bf16[256,3584]{0,1:T(8,128)(2,1)}, u32[]{:S(2)}, u32[]{:S(2)}) collective-permute-start(bf16[256,3584]{0,1:T(8,128)(2,1)} %get-tuple-element.20), channel_id=1, source_target_pairs={{0,1},{1,0},{2,3},{3,2},{4,5},{5,4},{6,7},{7,6}} | collective-permute-start | bytes 5505032 | tf_op jit(solution)/shard_map/ppermute | solution.py:19
  1562.5 111.6 %collective-permute-start.29 = (bf16[256,3584]{0,1:T(8,128)(2,1)}, bf16[256,3584]{0,1:T(8,128)(2,1)}, u32[]{:S(2)}, u32[]{:S(2)}) collective-permute-start(bf16[256,3584]{0,1:T(8,128)(2,1)} %get-tuple-element.21), channel_id=1, source_target_pairs={{0,2},{2,0},{1,3},{3,1},{4,6},{6,4},{5,7},{7,5}} | collective-permute-start | bytes 5505032 | tf_op jit(solution)/shard_map/ppermute | solution.py:25
  1595.4 117.0 %collective-permute-start.30 = (bf16[256,3584]{0,1:T(8,128)(2,1)}, bf16[256,3584]{0,1:T(8,128)(2,1)}, u32[]{:S(2)}, u32[]{:S(2)}) collective-permute-start(bf16[256,3584]{0,1:T(8,128)(2,1)} %get-tuple-element.22), channel_id=1, source_target_pairs={{0,3},{1,2},{2,1},{3,0},{4,7},{5,6},{6,5},{7,4}} | collective-permute-start | bytes 5505032 | tf_op jit(solution)/shard_map/ppermute | solution.py:28
  1633.8 82.8 %collective-permute-start.31 = (bf16[256,3584]{0,1:T(8,128)(2,1)}, bf16[256,3584]{0,1:T(8,128)(2,1)S(1)}, u32[]{:S(2)}, u32[]{:S(2)}) collective-permute-start(bf16[256,3584]{0,1:T(8,128)(2,1)} %get-tuple-element.22), channel_id=1, source_target_pairs={{0,1},{1,0},{2,3},{3,2},{4,5},{5,4},{6,7},{7,6}} | collective-permute-start | bytes 5505032 | tf_op jit(solution)/shard_map/ppermute | solution.py:19
  1865.5 211.9 %collective-permute-start.28 = (f32[512,4096]{1,0:T(8,128)}, f32[512,4096]{1,0:T(8,128)}, u32[]{:S(2)}, u32[]{:S(2)}) collective-permute-start(f32[512,4096]{1,0:T(8,128)} %convolution_add_fusion), channel_id=1, source_target_pairs={{0,4},{4,0},{1,5},{5,1},{2,6},{6,2},{3,7},{7,3}} | collective-permute-start | bytes 25165832 | tf_op jit(solution)/shard_map/ppermute | solution.py:22
  1986.9 241.3 %collective-permute-start.21 = (f32[512,4096]{1,0:T(8,128)}, f32[512,4096]{1,0:T(8,128)}, u32[]{:S(2)}, u32[]{:S(2)}) collective-permute-start(f32[512,4096]{1,0:T(8,128)} %convolution_add_fusion.1), channel_id=1, source_target_pairs={{0,4},{4,0},{1,5},{5,1},{2,6},{6,2},{3,7},{7,3}} | collective-permute-start | bytes 25165832 | tf_op jit(solution)/shard_map/ppermute | solution.py:22
  (47 other events, 1849.8 us)

commit v2 on v1

--- a/solution.py
+++ b/solution.py
@@ -65,7 +65,8 @@
         def both(v):
             return after(jnp.concatenate([v, to_core(v)], 0))
 
-        rows_own = {'A': both(x), 'B': both(x_y)}
+        x_own = both(x)
+        rows_own = {'A': x_own, 'B': both(x_y)}
         rows_oth = {'A': both(x_o), 'B': both(xo_y)}
 
         part_up = {'A': [], 'B': []}
@@ -97,39 +98,58 @@
             step = rows // sum(shares)
             blocks += [(name, step * sum(shares[:k]), step * s) for k, s in enumerate(shares)]
 
+        every = list(range(len(CHUNKS)))
+        final = len(blocks) - 1
         h_own, h_recv, arrived = [], [], []
         for i, (name, start, size) in enumerate(blocks):
             def part(chunks, base):
                 return cat([hid[name][j][base + start:base + start + size] for j in chunks], 1)
 
-            every = list(range(len(CHUNKS)))
-            groups = [every[:-1], every[-1:]] if i == 0 else [every]
-            own, core, xs, ds = [], [], [], []
-            for chunks in groups:
-                mine, theirs = part(chunks, 0), part(chunks, rows)
-                if i >= 2:
-                    mine, theirs = after((mine, theirs), arrived[i - 2])
-                xs.append(to_x(mine))
-                ds.append(to_diag(theirs))
-                core.append(to_core(theirs))
-                own.append(mine)
+            x_groups = d_groups = [every]
+            if i == 0:
+                x_groups = d_groups = [every[:-1], every[-1:]]
+            if i == final:
+                x_groups = [every[:2], every[2:]]
+
+            def send(groups, base, *movers):
+                sent, got = [], [[] for _ in movers]
+                for chunks in groups:
+                    piece = part(chunks, base)
+                    sent.append(piece)
+                    held = after(piece, arrived[i - 2]) if i >= 2 else piece
+                    for k, (mover, source) in enumerate(movers):
+                        got[k].append(mover(held if source else piece))
+                return sent, got
+
+            own, (xs,) = send(x_groups, 0, (to_x, True))
+            _, (ds, core) = send(d_groups, rows, (to_diag, True), (to_core, False))
             arrived.append((xs[-1], ds[-1]))
             h_own.append(after(jnp.concatenate([*own, *core], 1)))
-            h_recv.append(after(jnp.concatenate([*xs, *ds], 1)))
+            h_recv.append((xs, ds, x_groups))
 
         from_y = []
         out = jnp.zeros(x.shape, x.dtype)
         for i, (name, start, size) in enumerate(blocks):
+            xs, ds, x_groups = h_recv[i]
             z_own = after(dot(h_own[i], w2_own))
+            if i != final:
+                recv = after(jnp.concatenate([*xs, *ds], 1))
+                z = dot(recv, w2_recv) + z_own
             if name == 'B':
-                z = dot(h_recv[i], w2_recv) + z_own
                 from_y.append((start, to_y(z)))
+                continue
+            base, rest = next((b, v) for b, v in reversed(from_y) if b <= start)
+            rest = rest[start - base:start - base + size]
+            if i != final:
+                z = (z + rest).astype(x.dtype)
             else:
-                base, rest = next((b, v) for b, v in reversed(from_y) if b <= start)
-                z = (dot(h_recv[i], w2_recv) + z_own) + rest[start - base:start - base + size]
-                z = z.astype(x.dtype)
-                z = jnp.where(cx == 0, z, jnp.roll(z, depth // 2, 1))
-                out = lax.dynamic_update_slice(out, z, (start, 0))
+                z = after((dot(ds[0], w2_recv[half:]) + z_own) + rest)
+                for g, (piece, chunks) in enumerate(zip(xs, x_groups)):
+                    row = starts[chunks[0]]
+                    z = dot(piece, w2_recv[row:row + piece.shape[1]]) + z
+                    z = after(z) if g == 0 else z.astype(x.dtype)
+            z = jnp.where(cx == 0, z, jnp.roll(z, depth // 2, 1))
+            out = lax.dynamic_update_slice(out, z, (start, 0))
         return out
 
     return jax.shard_map(local_mlp, mesh=mesh, in_specs=(data_spec, up_spec, down_spec), out_specs=data_spec, check_vma=False)

time: 2260 us -> 2200 us (0.973)
  waiting for transfers between devices: 1110 us -> 1060 us
    ppermute x4, waiting for transfers between devices: 96.4 us -> 327 us  [to_y(): return lax.ppermute(v, 'cz', swap)]
    ppermute x6, waiting for transfers between devices: 279 us -> 116 us  [to_diag(): return lax.ppermute(v, ('cy', 'cx'), [(0, 3), (1, 2), (2, 1), (3, 0)])]
    ppermute x11 -> x12, waiting for transfers between devices: 740 us -> 611 us  [to_x(): return lax.ppermute(v, 'cy', swap)]
    dot_general x26 -> x28, matrix products: 698 us -> 706 us  [dot(): return jnp.dot(a, b, preferred_element_type=jnp.float32)]
  transfers between devices with their start and end apart: 32 -> 33, of which waited for: 15 -> 15; matrix products, arithmetic and copies ran while one was open for 41% -> 49% of each run, Pallas kernels for 0% -> 0%
where the time goes in v2:
time: 2200 us; the launch traced here: 2190 us
  waiting for transfers between devices  1060 us (48%)
  matrix products  706 us (32%)
  local copies, waits for them, and re-layouts  285 us (13%)
  other arithmetic  119 us (5%)
  starting transfers between devices  25.1 us (1%)
    dot_general x28, matrix products, dot(): return jnp.dot(a, b, preferred_element_type=jnp.float32)  706 us
    ppermute x12, waiting for transfers between devices, to_x(): return lax.ppermute(v, 'cy', swap)  611 us
    ppermute x4, waiting for transfers between devices, to_y(): return lax.ppermute(v, 'cz', swap)  327 us
    ppermute x6, waiting for transfers between devices, to_diag(): return lax.ppermute(v, ('cy', 'cx'), [(0, 3), (1, 2), (2, 1), (3, 0)])  116 us
    dynamic_update_slice x5, local copies, waits for them, and re-layouts, down(): buf = lax.dynamic_update_slice(buf, piece, (r * half, c * width))  115 us
    optimization_barrier x8, local copies, waits for them, and re-layouts, after(): return lax.optimization_barrier((v, *deps))[0]  65.9 us
  transfers between devices with their start and end apart: 33, of which 15 were waited for; matrix products, arithmetic and copies ran while one was open for 49% of the time, Pallas kernels for 0%

profile of v2, /device:TPU:0, one launch (start us, length us, event | category | flops | bytes accessed | tf_op | source)
XLA Modules:
  0.0 2191.6 jit_solution(14273468647126954775)
XLA Ops:
  35.5 23.6 %fusion.56 = f32[2048,1024]{1,0:T(8,128)} fusion(bf16[2048,4096]{1,0:T(8,128)(2,1)S(1)} %pad_maximum_fusion.1, bf16[4096,7168]{1,0:T(8,128)(2,1)} %param.4, s32[]{:T(128)S(6)} %select_n.70), kind=kOutput, calls=%fused_computation.73 | convolution fusion | flops 17179869184 | bytes 33554436 | tf_op jit(solution)/shard_map/dot_general | solution.py:37
  59.1 125.7 %collective-permute-done.9 = bf16[1024,4096]{1,0:T(8,128)(2,1)} collective-permute-done((bf16[1024,4096]{1,0:T(8,128)(2,1)}, bf16[1024,4096]{1,0:T(8,128)(2,1)}, u32[]{:S(2)}, u32[]{:S(2)}) %collective-permute-start.9) | collective-permute-done | bytes 8388640 | tf_op jit(solution)/shard_map/ppermute | solution.py:22
  211.9 24.1 %fusion.64 = f32[2048,1024]{1,0:T(8,128)} fusion(bf16[2048,4096]{1,0:T(8,128)(2,1)} %copy-done.2, bf16[4096,7168]{1,0:T(8,128)(2,1)} %param.4, s32[]{:T(128)S(6)} %select_n.66), kind=kOutput, calls=%fused_computation.81 | convolution fusion | flops 17179869184 | bytes 33554436 | tf_op jit(solution)/shard_map/dot_general | solution.py:37
  245.2 24.0 %fusion.60 = f32[2048,1024]{1,0:T(8,128)} fusion(bf16[2048,4096]{1,0:T(8,128)(2,1)} %copy-done.2, bf16[4096,7168]{1,0:T(8,128)(2,1)} %param.4, s32[]{:T(128)S(6)} %select_n.68), kind=kOutput, calls=%fused_computation.77 | convolution fusion | flops 17179869184 | bytes 33554436 | tf_op jit(solution)/shard_map/dot_general | solution.py:37
  280.0 86.7 %collective-permute-done.2 = bf16[4096,1024]{1,0:T(8,128)(2,1)} collective-permute-done((bf16[4096,1024]{1,0:T(8,128)(2,1)}, bf16[4096,1024]{1,0:T(8,128)(2,1)}, u32[]{:S(2)}, u32[]{:S(2)}) %collective-permute-start.2) | collective-permute-done | bytes 8388640 | tf_op jit(solution)/shard_map/ppermute | solution.py:25
  499.7 46.8 %collective-permute-done.4 = bf16[4096,1024]{1,0:T(8,128)(2,1)} collective-permute-done((bf16[4096,1024]{1,0:T(8,128)(2,1)}, bf16[4096,1024]{1,0:T(8,128)(2,1)}, u32[]{:S(2)}, u32[]{:S(2)}) %collective-permute-start.4) | collective-permute-done | bytes 8388640 | tf_op jit(solution)/shard_map/ppermute | solution.py:25
  549.3 26.9 %fusion.13 = bf16[2048,1024]{0,1:T(8,128)(2,1)} fusion(f32[2048,1024]{0,1:T(8,128)} %copy.4, bf16[2048,4096]{1,0:T(8,128)(2,1)} %pad_maximum_fusion, bf16[4096,1024]{1,0:T(8,128)(2,1)} %collective-permute-done.2), kind=kOutput, calls=%fused_computation.29 | convolution fusion | flops 17202937856 | bytes 37748736 | tf_op jit(solution)/shard_map/dot_general | solution.py:37
  579.1 26.7 %fusion.21 = bf16[2048,1024]{0,1:T(8,128)(2,1)} fusion(f32[2048,1024]{0,1:T(8,128)} %copy.5, bf16[2048,4096]{1,0:T(8,128)(2,1)} %pad_maximum_fusion, bf16[4096,1024]{1,0:T(8,128)(2,1)} %collective-permute-done.4), kind=kOutput, calls=%fused_computation.37 | convolution fusion | flops 17202937856 | bytes 37748736 | tf_op jit(solution)/shard_map/dot_general | solution.py:37
  608.9 117.3 %collective-permute-done.5 = bf16[4096,1024]{1,0:T(8,128)(2,1)} collective-permute-done((bf16[4096,1024]{1,0:T(8,128)(2,1)}, bf16[4096,1024]{1,0:T(8,128)(2,1)}, u32[]{:S(2)}, u32[]{:S(2)}) %collective-permute-start.5) | collective-permute-done | bytes 8388640 | tf_op jit(solution)/shard_map/ppermute | solution.py:25
  726.3 26.9 %fusion.29 = bf16[2048,1024]{0,1:T(8,128)(2,1)} fusion(f32[2048,1024]{0,1:T(8,128)} %copy.6, bf16[2048,4096]{1,0:T(8,128)(2,1)} %pad_maximum_fusion, bf16[4096,1024]{1,0:T(8,128)(2,1)} %collective-permute-done.5), kind=kOutput, calls=%fused_computation.45 | convolution fusion | flops 17202937856 | bytes 37748736 | tf_op jit(solution)/shard_map/dot_general | solution.py:37
  767.2 48.3 %collective-permute-done.6 = bf16[4096,512]{1,0:T(8,128)(2,1)} collective-permute-done((bf16[4096,512]{1,0:T(8,128)(2,1)}, bf16[4096,512]{1,0:T(8,128)(2,1)}, u32[]{:S(2)}, u32[]{:S(2)}) %collective-permute-start.6) | collective-permute-done | bytes 4194336 | tf_op jit(solution)/shard_map/ppermute | solution.py:25
  857.1 24.7 %fusion.123 = f32[2048,1024]{0,1:T(8,128)} fusion(bf16[2048,4096]{1,0:T(8,128)(2,1)} %pad_maximum_fusion.2, bf16[4096,1024]{1,0:T(8,128)(2,1)} %collective-permute-done.2), kind=kOutput, calls=%fused_computation.185 | convolution fusion | flops 17179869184 | bytes 33554432 | tf_op jit(solution)/shard_map/dot_general | solution.py:37
  890.1 24.4 %fusion.124 = f32[2048,1024]{0,1:T(8,128)} fusion(bf16[2048,4096]{1,0:T(8,128)(2,1)} %pad_maximum_fusion.2, bf16[4096,1024]{1,0:T(8,128)(2,1)} %collective-permute-done.4), kind=kOutput, calls=%fused_computation.186 | convolution fusion | flops 17179869184 | bytes 33554432 | tf_op jit(solution)/shard_map/dot_general | solution.py:37
  938.2 24.3 %fusion.125 = f32[2048,1024]{0,1:T(8,128)} fusion(bf16[2048,4096]{1,0:T(8,128)(2,1)} %pad_maximum_fusion.2, bf16[4096,1024]{1,0:T(8,128)(2,1)} %collective-permute-done.5), kind=kOutput, calls=%fused_computation.187 | convolution fusion | flops 17179869184 | bytes 33554432 | tf_op jit(solution)/shard_map/dot_general | solution.py:37
  1052.8 25.3 %dynamic_update_slice.37 = bf16[7168,4096]{1,0:T(8,128)(2,1)} pad(bf16[3584,2048]{1,0:T(8,128)(2,1)} %get-tuple-element.32, bf16[]{:T(256)} %constant.47.clone.1), padding=0_3584x0_2048 | pad | bytes 73400320 | tf_op jit(solution)/shard_map/dynamic_update_slice | solution.py:90
  1086.7 56.9 %collective-permute-done.17 = bf16[512,3072]{0,1:T(8,128)(2,1)} collective-permute-done((bf16[512,3072]{0,1:T(8,128)(2,1)}, bf16[512,3072]{0,1:T(8,128)(2,1)}, u32[]{:S(2)}, u32[]{:S(2)}) %collective-permute-start.17) | collective-permute-done | bytes 3145760 | tf_op jit(solution)/shard_map/ppermute | solution.py:25
  1172.4 132.0 %collective-permute-done.22 = bf16[512,3584]{0,1:T(8,128)(2,1)} collective-permute-done((bf16[512,3584]{0,1:T(8,128)(2,1)S(1)}, bf16[512,3584]{0,1:T(8,128)(2,1)}, u32[]{:S(2)}, u32[]{:S(2)}) %collective-permute-start.22) | collective-permute-done | bytes 3670048 | tf_op jit(solution)/shard_map/ppermute | solution.py:25
  1312.4 70.6 %collective-permute-done.13 = bf16[512,3584]{0,1:T(8,128)(2,1)} collective-permute-done((bf16[512,3584]{0,1:T(8,128)(2,1)}, bf16[512,3584]{0,1:T(8,128)(2,1)}, u32[]{:S(2)}, u32[]{:S(2)}) %collective-permute-start.13) | collective-permute-done | bytes 3670048 | tf_op jit(solution)/shard_map/ppermute | solution.py:25
  1383.0 78.2 %collective-permute-done.14 = bf16[512,3584]{0,1:T(8,128)(2,1)} collective-permute-done((bf16[512,3584]{0,1:T(8,128)(2,1)}, bf16[512,3584]{0,1:T(8,128)(2,1)}, u32[]{:S(2)}, u32[]{:S(2)}) %collective-permute-start.14) | collective-permute-done | bytes 3670048 | tf_op jit(solution)/shard_map/ppermute | solution.py:28
  1469.9 31.1 %collective-permute-done.24 = bf16[256,3584]{0,1:T(8,128)(2,1)} collective-permute-done((bf16[256,3584]{0,1:T(8,128)(2,1)}, bf16[256,3584]{0,1:T(8,128)(2,1)}, u32[]{:S(2)}, u32[]{:S(2)}) %collective-permute-start.24) | collective-permute-done | bytes 1835040 | tf_op jit(solution)/shard_map/ppermute | solution.py:25
  1501.8 38.1 %collective-permute-done.25 = bf16[256,3584]{0,1:T(8,128)(2,1)} collective-permute-done((bf16[256,3584]{0,1:T(8,128)(2,1)}, bf16[256,3584]{0,1:T(8,128)(2,1)}, u32[]{:S(2)}, u32[]{:S(2)}) %collective-permute-start.25) | collective-permute-done | bytes 1835040 | tf_op jit(solution)/shard_map/ppermute | solution.py:28
  1611.2 25.3 %fusion.129 = f32[256,4096]{1,0:T(8,128)} fusion(bf16[256,7168]{0,1:T(8,128)(2,1)S(1)} %constant_dynamic-update-slice_fusion.21, bf16[7168,4096]{1,0:T(8,128)(2,1)} %get-tuple-element.26), kind=kOutput, calls=%fused_computation.191 | convolution fusion | flops 15032385536 | bytes 66584576 | tf_op jit(solution)/shard_map/dot_general | solution.py:37
  1636.4 39.6 %fusion.128 = f32[512,4096]{1,0:T(8,128)} fusion(bf16[512,7168]{0,1:T(8,128)(2,1)} %constant_dynamic-update-slice_fusion.16, bf16[7168,4096]{1,0:T(8,128)(2,1)} %get-tuple-element.26), kind=kOutput, calls=%fused_computation.190 | convolution fusion | flops 30064771072 | bytes 74448896 | tf_op jit(solution)/shard_map/dot_general | solution.py:37
  1676.1 39.7 %fusion.126 = f32[512,4096]{1,0:T(8,128)} fusion(bf16[512,7168]{0,1:T(8,128)(2,1)} %constant_dynamic-update-slice_fusion.5, bf16[7168,4096]{1,0:T(8,128)(2,1)} %get-tuple-element.26), kind=kOutput, calls=%fused_computation.188 | convolution fusion | flops 30064771072 | bytes 74448896 | tf_op jit(solution)/shard_map/dot_general | solution.py:37
  1715.8 40.2 %convolution_add_fusion.1 = f32[512,4096]{1,0:T(8,128)} fusion(f32[512,4096]{1,0:T(8,128)} %fusion.126, bf16[512,7168]{0,1:T(8,128)(2,1)} %pad_maximum_fusion.5, bf16[7168,4096]{1,0:T(8,128)(2,1)} %get-tuple-element.25), kind=kOutput, calls=%fused_computation.89 | convolution fusion | flops 30066868224 | bytes 82837504 | tf_op jit(solution)/shard_map/dot_general | solution.py:37
  1756.3 40.5 %convolution_add_fusion = f32[512,4096]{1,0:T(8,128)} fusion(f32[512,4096]{1,0:T(8,128)} %fusion.128, bf16[512,7168]{0,1:T(8,128)(2,1)} %pad_maximum_fusion.6, bf16[7168,4096]{1,0:T(8,128)(2,1)} %get-tuple-element.25), kind=kOutput, calls=%fused_computation.88 | convolution fusion | flops 30066868224 | bytes 82837504 | tf_op jit(solution)/shard_map/dot_general | solution.py:37
  1796.8 25.6 %fusion.127 = f32[256,4096]{1,0:T(8,128)} fusion(bf16[256,7168]{0,1:T(8,128)(2,1)} %constant_dynamic-update-slice_fusion.11, bf16[7168,4096]{1,0:T(8,128)(2,1)} %get-tuple-element.26), kind=kOutput, calls=%fused_computation.189 | convolution fusion | flops 15032385536 | bytes 66584576 | tf_op jit(solution)/shard_map/dot_general | solution.py:37
  1824.1 41.0 %fusion.122 = f32[512,4096]{1,0:T(8,128)S(1)} fusion(bf16[512,7168]{0,1:T(8,128)(2,1)} %copy-done.31, bf16[7168,4096]{1,0:T(8,128)(2,1)} %get-tuple-element.26), kind=kOutput, calls=%fused_computation.184 | convolution fusion | flops 30064771072 | bytes 74448896 | tf_op jit(solution)/shard_map/dot_general | solution.py:37
  1865.1 39.8 %fusion.121 = f32[512,4096]{1,0:T(8,128)} fusion(bf16[512,7168]{0,1:T(8,128)(2,1)} %pad_maximum_fusion.4, bf16[7168,4096]{1,0:T(8,128)(2,1)} %get-tuple-element.25), kind=kOutput, calls=%fused_computation.183 | convolution fusion | flops 30064771072 | bytes 74448896 | tf_op jit(solution)/shard_map/dot_general | solution.py:37
  1904.9 34.8 %collective-permute-done.21 = f32[512,4096]{1,0:T(8,128)} collective-permute-done((f32[512,4096]{1,0:T(8,128)}, f32[512,4096]{1,0:T(8,128)}, u32[]{:S(2)}, u32[]{:S(2)}) %collective-permute-start.21) | collective-permute-done | bytes 8388640 | tf_op jit(solution)/shard_map/ppermute | solution.py:22
  1953.2 165.5 %collective-permute-done.28 = f32[512,4096]{1,0:T(8,128)} collective-permute-done((f32[512,4096]{1,0:T(8,128)}, f32[512,4096]{1,0:T(8,128)}, u32[]{:S(2)}, u32[]{:S(2)}) %collective-permute-start.28) | collective-permute-done | bytes 8388640 | tf_op jit(solution)/shard_map/ppermute | solution.py:22
  2161.7 25.1 %fusion.79 = bf16[256,4096]{1,0:T(8,128)(2,1)S(1)} fusion(f32[256,4096]{1,0:T(8,128)S(1)} %copy-done.1, bf16[256,7168]{0,1:T(8,128)(2,1)S(1)} %copy-done, bf16[7168,4096]{1,0:T(8,128)(2,1)} %get-tuple-element.25, f32[512,4096]{1,0:T(8,128)} %collective-permute-done.28), kind=kOutput, calls=%fused_computation.96 | convolution fusion | flops 15035531264 | bytes 72876032 | tf_op jit(solution)/shard_map/dot_general | solution.py:37
  (211 shorter events, 591.2 us)
Async XLA Ops:
  0.0 26.9 %collective-permute-start.3 = (bf16[1024,4096]{1,0:T(8,128)(2,1)}, bf16[1024,4096]{1,0:T(8,128)(2,1)}, u32[]{:S(2)}, u32[]{:S(2)}) collective-permute-start(bf16[1024,4096]{1,0:T(8,128)(2,1)} %param.3), channel_id=1, source_target_pairs={{0,1},{1,0},{2,3},{3,2},{4,5},{5,4},{6,7},{7,6}} | collective-permute-start | bytes 25165832 | tf_op jit(solution)/shard_map/ppermute | solution.py:19
  0.8 183.9 %collective-permute-start.9 = (bf16[1024,4096]{1,0:T(8,128)(2,1)}, bf16[1024,4096]{1,0:T(8,128)(2,1)}, u32[]{:S(2)}, u32[]{:S(2)}) collective-permute-start(bf16[1024,4096]{1,0:T(8,128)(2,1)} %param.3), channel_id=1, source_target_pairs={{0,4},{4,0},{1,5},{5,1},{2,6},{6,2},{3,7},{7,3}} | collective-permute-start | bytes 25165832 | tf_op jit(solution)/shard_map/ppermute | solution.py:22
  3.3 275.0 %collective-permute-start = (bf16[1024,4096]{1,0:T(8,128)(2,1)}, bf16[1024,4096]{1,0:T(8,128)(2,1)}, u32[]{:S(2)}, u32[]{:S(2)}) collective-permute-start(bf16[1024,4096]{1,0:T(8,128)(2,1)} %param.3), channel_id=1, source_target_pairs={{0,2},{2,0},{1,3},{3,1},{4,6},{6,4},{5,7},{7,5}} | collective-permute-start | bytes 25165832 | tf_op jit(solution)/shard_map/ppermute | solution.py:25
  21.9 344.9 %collective-permute-start.2 = (bf16[4096,1024]{1,0:T(8,128)(2,1)}, bf16[4096,1024]{1,0:T(8,128)(2,1)}, u32[]{:S(2)}, u32[]{:S(2)}) collective-permute-start(bf16[4096,1024]{1,0:T(8,128)(2,1)} %get-tuple-element.35), channel_id=1, source_target_pairs={{0,2},{2,0},{1,3},{3,1},{4,6},{6,4},{5,7},{7,5}} | collective-permute-start | bytes 25165832 | tf_op jit(solution)/shard_map/ppermute | solution.py:25
  22.4 1521.6 %collective-permute-start.15 = (bf16[14336,2048]{1,0:T(8,128)(2,1)}, bf16[14336,2048]{1,0:T(8,128)(2,1)}, u32[]{:S(2)}, u32[]{:S(2)}) collective-permute-start(bf16[14336,2048]{1,0:T(8,128)(2,1)} %param.5), channel_id=1, source_target_pairs={{0,1},{1,0},{2,3},{3,2},{4,5},{5,4},{6,7},{7,6}} | collective-permute-start | bytes 176160768 | tf_op jit(solution)/shard_map/ppermute | solution.py:19
  184.8 184.0 %collective-permute-start.10 = (bf16[1024,4096]{1,0:T(8,128)(2,1)}, bf16[1024,4096]{1,0:T(8,128)(2,1)}, u32[]{:S(2)}, u32[]{:S(2)}) collective-permute-start(bf16[1024,4096]{1,0:T(8,128)(2,1)} %collective-permute-done.9), channel_id=1, source_target_pairs={{0,1},{1,0},{2,3},{3,2},{4,5},{5,4},{6,7},{7,6}} | collective-permute-start | bytes 25165832 | tf_op jit(solution)/shard_map/ppermute | solution.py:19
  278.3 268.2 %collective-permute-start.4 = (bf16[4096,1024]{1,0:T(8,128)(2,1)}, bf16[4096,1024]{1,0:T(8,128)(2,1)}, u32[]{:S(2)}, u32[]{:S(2)}) collective-permute-start(bf16[4096,1024]{1,0:T(8,128)(2,1)} %get-tuple-element.15), channel_id=1, source_target_pairs={{0,2},{2,0},{1,3},{3,1},{4,6},{6,4},{5,7},{7,5}} | collective-permute-start | bytes 25165832 | tf_op jit(solution)/shard_map/ppermute | solution.py:25
  366.8 359.5 %collective-permute-start.5 = (bf16[4096,1024]{1,0:T(8,128)(2,1)}, bf16[4096,1024]{1,0:T(8,128)(2,1)}, u32[]{:S(2)}, u32[]{:S(2)}) collective-permute-start(bf16[4096,1024]{1,0:T(8,128)(2,1)} %get-tuple-element.16), channel_id=1, source_target_pairs={{0,2},{2,0},{1,3},{3,1},{4,6},{6,4},{5,7},{7,5}} | collective-permute-start | bytes 25165832 | tf_op jit(solution)/shard_map/ppermute | solution.py:25
  368.2 181.0 %collective-permute-start.7 = (bf16[1024,4096]{1,0:T(8,128)(2,1)}, bf16[1024,4096]{1,0:T(8,128)(2,1)}, u32[]{:S(2)}, u32[]{:S(2)}) collective-permute-start(bf16[1024,4096]{1,0:T(8,128)(2,1)} %collective-permute-done), channel_id=1, source_target_pairs={{0,4},{4,0},{1,5},{5,1},{2,6},{6,2},{3,7},{7,3}} | collective-permute-start | bytes 25165832 | tf_op jit(solution)/shard_map/ppermute | solution.py:22
  368.8 87.3 %collective-permute-start.1 = (bf16[1024,4096]{1,0:T(8,128)(2,1)}, bf16[1024,4096]{1,0:T(8,128)(2,1)S(1)}, u32[]{:S(2)}, u32[]{:S(2)}) collective-permute-start(bf16[1024,4096]{1,0:T(8,128)(2,1)} %collective-permute-done), channel_id=1, source_target_pairs={{0,1},{1,0},{2,3},{3,2},{4,5},{5,4},{6,7},{7,6}} | collective-permute-start | bytes 25165832 | tf_op jit(solution)/shard_map/ppermute | solution.py:19
  546.5 268.9 %collective-permute-start.6 = (bf16[4096,512]{1,0:T(8,128)(2,1)}, bf16[4096,512]{1,0:T(8,128)(2,1)}, u32[]{:S(2)}, u32[]{:S(2)}) collective-permute-start(bf16[4096,512]{1,0:T(8,128)(2,1)} %constant_dynamic-slice_fusion.2), channel_id=1, source_target_pairs={{0,2},{2,0},{1,3},{3,1},{4,6},{6,4},{5,7},{7,5}} | collective-permute-start | bytes 12582920 | tf_op jit(solution)/shard_map/ppermute | solution.py:25
  549.3 293.8 %collective-permute-start.8 = (bf16[1024,4096]{1,0:T(8,128)(2,1)}, bf16[1024,4096]{1,0:T(8,128)(2,1)}, u32[]{:S(2)}, u32[]{:S(2)}) collective-permute-start(bf16[1024,4096]{1,0:T(8,128)(2,1)} %collective-permute-done.7), channel_id=1, source_target_pairs={{0,1},{1,0},{2,3},{3,2},{4,5},{5,4},{6,7},{7,6}} | collective-permute-start | bytes 25165832 | tf_op jit(solution)/shard_map/ppermute | solution.py:19
  836.9 143.0 %collective-permute-start.26 = (bf16[256,3584]{0,1:T(8,128)(2,1)}, bf16[256,3584]{0,1:T(8,128)(2,1)}, u32[]{:S(2)}, u32[]{:S(2)}) collective-permute-start(bf16[256,3584]{0,1:T(8,128)(2,1)} %pad_maximum_fusion.15), channel_id=1, source_target_pairs={{0,1},{1,0},{2,3},{3,2},{4,5},{5,4},{6,7},{7,6}} | collective-permute-start | bytes 5505032 | tf_op jit(solution)/shard_map/ppermute | solution.py:19
  839.4 141.6 %collective-permute-start.32 = (bf16[256,3584]{0,1:T(8,128)(2,1)}, bf16[256,3584]{0,1:T(8,128)(2,1)}, u32[]{:S(2)}, u32[]{:S(2)}) collective-permute-start(bf16[256,3584]{0,1:T(8,128)(2,1)} %pad_maximum_fusion.16), channel_id=1, source_target_pairs={{0,1},{1,0},{2,3},{3,2},{4,5},{5,4},{6,7},{7,6}} | collective-permute-start | bytes 5505032 | tf_op jit(solution)/shard_map/ppermute | solution.py:19
  843.1 140.4 %collective-permute-start.16 = (bf16[512,3584]{0,1:T(8,128)(2,1)}, bf16[512,3584]{0,1:T(8,128)(2,1)}, u32[]{:S(2)}, u32[]{:S(2)}) collective-permute-start(bf16[512,3584]{0,1:T(8,128)(2,1)} %pad_maximum_fusion.8), channel_id=1, source_target_pairs={{0,1},{1,0},{2,3},{3,2},{4,5},{5,4},{6,7},{7,6}} | collective-permute-start | bytes 11010056 | tf_op jit(solution)/shard_map/ppermute | solution.py:19
  975.7 30.7 %collective-permute-start.20 = (bf16[512,512]{0,1:T(8,128)(2,1)S(1)}, bf16[512,512]{0,1:T(8,128)(2,1)S(1)}, u32[]{:S(2)}, u32[]{:S(2)}) collective-permute-start(bf16[512,512]{0,1:T(8,128)(2,1)S(1)} %get-tuple-element.97), channel_id=1, source_target_pairs={{0,1},{1,0},{2,3},{3,2},{4,5},{5,4},{6,7},{7,6}} | collective-permute-start | bytes 1572872 | tf_op jit(solution)/shard_map/ppermute | solution.py:19
  979.9 27.1 %collective-permute-start.12 = (bf16[512,512]{0,1:T(8,128)(2,1)S(1)}, bf16[512,512]{0,1:T(8,128)(2,1)}, u32[]{:S(2)}, u32[]{:S(2)}) collective-permute-start(bf16[512,512]{0,1:T(8,128)(2,1)S(1)} %get-tuple-element.97), channel_id=1, source_target_pairs={{0,3},{1,2},{2,1},{3,0},{4,7},{5,6},{6,5},{7,4}} | collective-permute-start | bytes 1572872 | tf_op jit(solution)/shard_map/ppermute | solution.py:28
  983.5 161.2 %collective-permute-start.19 = (bf16[512,3072]{0,1:T(8,128)(2,1)}, bf16[512,3072]{0,1:T(8,128)(2,1)}, u32[]{:S(2)}, u32[]{:S(2)}) collective-permute-start(bf16[512,3072]{0,1:T(8,128)(2,1)} %pad_maximum_fusion.13), channel_id=1, source_target_pairs={{0,1},{1,0},{2,3},{3,2},{4,5},{5,4},{6,7},{7,6}} | collective-permute-start | bytes 9437192 | tf_op jit(solution)/shard_map/ppermute | solution.py:19
  1005.4 143.7 %collective-permute-start.18 = (bf16[512,3072]{0,1:T(8,128)(2,1)}, bf16[512,3072]{0,1:T(8,128)(2,1)}, u32[]{:S(2)}, u32[]{:S(2)}) collective-permute-start(bf16[512,3072]{0,1:T(8,128)(2,1)} %pad_maximum_fusion.13), channel_id=1, source_target_pairs={{0,3},{1,2},{2,1},{3,0},{4,7},{5,6},{6,5},{7,4}} | collective-permute-start | bytes 9437192 | tf_op jit(solution)/shard_map/ppermute | solution.py:28
  1006.4 137.1 %collective-permute-start.17 = (bf16[512,3072]{0,1:T(8,128)(2,1)}, bf16[512,3072]{0,1:T(8,128)(2,1)}, u32[]{:S(2)}, u32[]{:S(2)}) collective-permute-start(bf16[512,3072]{0,1:T(8,128)(2,1)} %pad_maximum_fusion.12), channel_id=1, source_target_pairs={{0,2},{2,0},{1,3},{3,1},{4,6},{6,4},{5,7},{7,5}} | collective-permute-start | bytes 9437192 | tf_op jit(solution)/shard_map/ppermute | solution.py:25
  1007.2 143.4 %collective-permute-start.27 = (bf16[512,3584]{0,1:T(8,128)(2,1)}, bf16[512,3584]{0,1:T(8,128)(2,1)}, u32[]{:S(2)}, u32[]{:S(2)}) collective-permute-start(bf16[512,3584]{0,1:T(8,128)(2,1)} %pad_maximum_fusion.10), channel_id=1, source_target_pairs={{0,1},{1,0},{2,3},{3,2},{4,5},{5,4},{6,7},{7,6}} | collective-permute-start | bytes 11010056 | tf_op jit(solution)/shard_map/ppermute | solution.py:19
  1143.6 160.8 %collective-permute-start.23 = (bf16[512,3584]{0,1:T(8,128)(2,1)}, bf16[512,3584]{0,1:T(8,128)(2,1)}, u32[]{:S(2)}, u32[]{:S(2)}) collective-permute-start(bf16[512,3584]{0,1:T(8,128)(2,1)} %pad_maximum_fusion.10), channel_id=1, source_target_pairs={{0,3},{1,2},{2,1},{3,0},{4,7},{5,6},{6,5},{7,4}} | collective-permute-start | bytes 11010056 | tf_op jit(solution)/shard_map/ppermute | solution.py:28
  1144.7 159.7 %collective-permute-start.22 = (bf16[512,3584]{0,1:T(8,128)(2,1)S(1)}, bf16[512,3584]{0,1:T(8,128)(2,1)}, u32[]{:S(2)}, u32[]{:S(2)}) collective-permute-start(bf16[512,3584]{0,1:T(8,128)(2,1)S(1)} %pad_maximum_fusion.9), channel_id=1, source_target_pairs={{0,2},{2,0},{1,3},{3,1},{4,6},{6,4},{5,7},{7,5}} | collective-permute-start | bytes 11010056 | tf_op jit(solution)/shard_map/ppermute | solution.py:25
  1149.1 233.9 %collective-permute-start.13 = (bf16[512,3584]{0,1:T(8,128)(2,1)}, bf16[512,3584]{0,1:T(8,128)(2,1)}, u32[]{:S(2)}, u32[]{:S(2)}) collective-permute-start(bf16[512,3584]{0,1:T(8,128)(2,1)} %pad_maximum_fusion.7), channel_id=1, source_target_pairs={{0,2},{2,0},{1,3},{3,1},{4,6},{6,4},{5,7},{7,5}} | collective-permute-start | bytes 11010056 | tf_op jit(solution)/shard_map/ppermute | solution.py:25
  1150.6 310.6 %collective-permute-start.14 = (bf16[512,3584]{0,1:T(8,128)(2,1)}, bf16[512,3584]{0,1:T(8,128)(2,1)}, u32[]{:S(2)}, u32[]{:S(2)}) collective-permute-start(bf16[512,3584]{0,1:T(8,128)(2,1)} %pad_maximum_fusion.8), channel_id=1, source_target_pairs={{0,3},{1,2},{2,1},{3,0},{4,7},{5,6},{6,5},{7,4}} | collective-permute-start | bytes 11010056 | tf_op jit(solution)/shard_map/ppermute | solution.py:28
  1304.4 196.6 %collective-permute-start.24 = (bf16[256,3584]{0,1:T(8,128)(2,1)}, bf16[256,3584]{0,1:T(8,128)(2,1)}, u32[]{:S(2)}, u32[]{:S(2)}) collective-permute-start(bf16[256,3584]{0,1:T(8,128)(2,1)} %pad_maximum_fusion.14), channel_id=1, source_target_pairs={{0,2},{2,0},{1,3},{3,1},{4,6},{6,4},{5,7},{7,5}} | collective-permute-start | bytes 5505032 | tf_op jit(solution)/shard_map/ppermute | solution.py:25
  1305.9 234.0 %collective-permute-start.25 = (bf16[256,3584]{0,1:T(8,128)(2,1)}, bf16[256,3584]{0,1:T(8,128)(2,1)}, u32[]{:S(2)}, u32[]{:S(2)}) collective-permute-start(bf16[256,3584]{0,1:T(8,128)(2,1)} %pad_maximum_fusion.15), channel_id=1, source_target_pairs={{0,3},{1,2},{2,1},{3,0},{4,7},{5,6},{6,5},{7,4}} | collective-permute-start | bytes 5505032 | tf_op jit(solution)/shard_map/ppermute | solution.py:28
  1461.2 689.2 %collective-permute-start.29 = (bf16[256,1536]{0,1:T(8,128)(2,1)}, bf16[256,1536]{0,1:T(8,128)(2,1)}, u32[]{:S(2)}, u32[]{:S(2)}) collective-permute-start(bf16[256,1536]{0,1:T(8,128)(2,1)} %pad_maximum_fusion.18), channel_id=1, source_target_pairs={{0,2},{2,0},{1,3},{3,1},{4,6},{6,4},{5,7},{7,5}} | collective-permute-start | bytes 2359304 | tf_op jit(solution)/shard_map/ppermute | solution.py:25
  1462.7 673.8 %collective-permute-start.30 = (bf16[256,2048]{0,1:T(8,128)(2,1)}, bf16[256,2048]{0,1:T(8,128)(2,1)}, u32[]{:S(2)}, u32[]{:S(2)}) collective-permute-start(bf16[256,2048]{0,1:T(8,128)(2,1)} %pad_maximum_fusion.17), channel_id=1, source_target_pairs={{0,2},{2,0},{1,3},{3,1},{4,6},{6,4},{5,7},{7,5}} | collective-permute-start | bytes 3145736 | tf_op jit(solution)/shard_map/ppermute | solution.py:25
  1501.0 452.2 %collective-permute-start.31 = (bf16[256,3584]{0,1:T(8,128)(2,1)}, bf16[256,3584]{0,1:T(8,128)(2,1)}, u32[]{:S(2)}, u32[]{:S(2)}) collective-permute-start(bf16[256,3584]{0,1:T(8,128)(2,1)} %pad_maximum_fusion.16), channel_id=1, source_target_pairs={{0,3},{1,2},{2,1},{3,0},{4,7},{5,6},{6,5},{7,4}} | collective-permute-start | bytes 5505032 | tf_op jit(solution)/shard_map/ppermute | solution.py:28
  1756.1 183.6 %collective-permute-start.21 = (f32[512,4096]{1,0:T(8,128)}, f32[512,4096]{1,0:T(8,128)}, u32[]{:S(2)}, u32[]{:S(2)}) collective-permute-start(f32[512,4096]{1,0:T(8,128)} %convolution_add_fusion.1), channel_id=1, source_target_pairs={{0,4},{4,0},{1,5},{5,1},{2,6},{6,2},{3,7},{7,3}} | collective-permute-start | bytes 25165832 | tf_op jit(solution)/shard_map/ppermute | solution.py:22
  1822.4 296.4 %collective-permute-start.28 = (f32[512,4096]{1,0:T(8,128)}, f32[512,4096]{1,0:T(8,128)}, u32[]{:S(2)}, u32[]{:S(2)}) collective-permute-start(f32[512,4096]{1,0:T(8,128)} %convolution_add_fusion), channel_id=1, source_target_pairs={{0,4},{4,0},{1,5},{5,1},{2,6},{6,2},{3,7},{7,3}} | collective-permute-start | bytes 25165832 | tf_op jit(solution)/shard_map/ppermute | solution.py:22
  (41 other events, 1088.4 us)

commit v3 on v2

--- a/solution.py
+++ b/solution.py
@@ -1,12 +1,53 @@
 import jax
 import jax.numpy as jnp
 from jax import lax
+from jax.experimental import pallas as pl
+from jax.experimental.pallas import tpu as pltpu
 from jax.sharding import PartitionSpec as P
 
 
 CHUNKS = (2, 2, 2, 1)
 B_BLOCKS = (2, 2)
 A_BLOCKS = (2, 1, 1)
+TAIL_TILES = 8
+
+
+def tail_dot(shift, h, w, w_blocks, terms, out=None, out_row=0):
+    size, width = h.shape[0], w.shape[1]
+    tile = width // TAIL_TILES
+    rows = h.shape[1] // len(w_blocks)
+    n_w, n_t = len(w_blocks), len(terms)
+
+    def kernel(shift_ref, h_ref, *refs):
+        acc = refs[n_w][...]
+        for t in refs[n_w + 1:n_w + n_t]:
+            acc = acc + t[...]
+        for k in range(n_w):
+            acc = acc + jnp.dot(h_ref[:, k * rows:(k + 1) * rows], refs[k][...], preferred_element_type=jnp.float32)
+        refs[-1][...] = acc.astype(refs[-1].dtype)
+
+    in_specs = [pl.BlockSpec((size, h.shape[1]), lambda n, c: (0, 0))]
+    in_specs += [pl.BlockSpec((rows, tile), lambda n, c, b=b: (b, n)) for b in w_blocks]
+    in_specs += [pl.BlockSpec((size, tile), lambda n, c, b=b: (b, n)) for _, b in terms]
+    args = [h, *([w] * n_w), *(t for t, _ in terms)]
+    if out is None:
+        out_shape = jax.ShapeDtypeStruct((size, width), jnp.float32)
+        out_spec, aliases = pl.BlockSpec((size, tile), lambda n, c: (0, n)), {}
+    else:
+        in_specs.append(pl.BlockSpec(memory_space=pl.ANY))
+        args.append(out)
+        out_shape = jax.ShapeDtypeStruct(out.shape, out.dtype)
+        out_spec = pl.BlockSpec((size, tile), lambda n, c: (out_row // size, lax.rem(n + c[0], TAIL_TILES)))
+        aliases = {len(args): 0}
+    return pl.pallas_call(
+        kernel,
+        grid_spec=pltpu.PrefetchScalarGridSpec(
+            num_scalar_prefetch=1, grid=(TAIL_TILES,), in_specs=in_specs, out_specs=out_spec),
+        out_shape=out_shape,
+        input_output_aliases=aliases,
+        cost_estimate=pl.CostEstimate(
+            flops=2 * size * h.shape[1] * width, bytes_accessed=2 * h.shape[1] * width, transcendentals=0),
+    )(shift, *args)
 
 
 def solution(mesh):
@@ -139,17 +180,20 @@
                 from_y.append((start, to_y(z)))
                 continue
             base, rest = next((b, v) for b, v in reversed(from_y) if b <= start)
-            rest = rest[start - base:start - base + size]
             if i != final:
-                z = (z + rest).astype(x.dtype)
-            else:
-                z = after((dot(ds[0], w2_recv[half:]) + z_own) + rest)
-                for g, (piece, chunks) in enumerate(zip(xs, x_groups)):
-                    row = starts[chunks[0]]
-                    z = dot(piece, w2_recv[row:row + piece.shape[1]]) + z
-                    z = after(z) if g == 0 else z.astype(x.dtype)
-            z = jnp.where(cx == 0, z, jnp.roll(z, depth // 2, 1))
-            out = lax.dynamic_update_slice(out, z, (start, 0))
+                z = z + rest[start - base:start - base + size]
+                z = z.astype(x.dtype)
+                z = jnp.where(cx == 0, z, jnp.roll(z, depth // 2, 1))
+                out = lax.dynamic_update_slice(out, z, (start, 0))
+                continue
+            shift = jnp.full((1,), cx * (TAIL_TILES // 2), jnp.int32)
+            z = tail_dot(shift, ds[0], w2_recv, [1], [(z_own, 0), (rest, (start - base) // size)])
+            for g, (piece, chunks) in enumerate(zip(xs, x_groups)):
+                first, count = starts[chunks[0]] // unit, piece.shape[1] // unit
+                if g == 0:
+                    z = tail_dot(shift, piece, w2_recv, list(range(first, first + count)), [(z, 0)])
+                else:
+                    out = tail_dot(shift, piece, w2_recv, list(range(first, first + count)), [(z, 0)], out, start)
         return out
 
     return jax.shard_map(local_mlp, mesh=mesh, in_specs=(data_spec, up_spec, down_spec), out_specs=data_spec, check_vma=False)

time: 2200 us -> 2210 us (level)
  waiting for transfers between devices: 1060 us -> 1160 us
  local copies, waits for them, and re-layouts: 285 us -> 214 us
  matrix products: 706 us -> 654 us
  Pallas kernels: 0 us -> 42.6 us
    ppermute x12, waiting for transfers between devices: 611 us -> 683 us  [to_x(): return lax.ppermute(v, 'cy', swap)]
    optimization_barrier x8 -> x0, local copies, waits for them, and re-layouts: 65.9 us -> none  [after(): return lax.optimization_barrier((v, *deps))[0]]
    dot_general x28 -> x25, matrix products: 706 us -> 654 us  [dot(): return jnp.dot(a, b, preferred_element_type=jnp.float32)]
    pallas_call x0 -> x3, Pallas kernels: none -> 42.6 us  [tail_dot(): pl.pallas_call(kernel, grid_spec=pltpu.PrefetchScalarGridSpec(num_scalar_...]
    ppermute x4, waiting for transfers between devices: 327 us -> 356 us  [to_y(): return lax.ppermute(v, 'cz', swap)]
  transfers between devices with their start and end apart: 33 -> 33, of which waited for: 15 -> 15; matrix products, arithmetic and copies ran while one was open for 49% -> 44% of each run, Pallas kernels for 0% -> 1%
where the time goes in v3:
time: 2210 us; the launch traced here: 2200 us
  waiting for transfers between devices  1160 us (52%)
  matrix products  654 us (30%)
  local copies, waits for them, and re-layouts  214 us (10%)
  other arithmetic  107 us (5%)
  Pallas kernels  42.6 us (2%)
  starting transfers between devices  25.3 us (1%)
    ppermute x12, waiting for transfers between devices, to_x(): return lax.ppermute(v, 'cy', swap)  683 us
    dot_general x25, matrix products, dot(): return jnp.dot(a, b, preferred_element_type=jnp.float32)  654 us
    ppermute x4, waiting for transfers between devices, to_y(): return lax.ppermute(v, 'cz', swap)  356 us
    ppermute x6, waiting for transfers between devices, to_diag(): return lax.ppermute(v, ('cy', 'cx'), [(0, 3), (1, 2), (2, 1), (3, 0)])  117 us
    dynamic_update_slice x5, local copies, waits for them, and re-layouts, down(): buf = lax.dynamic_update_slice(buf, piece, (r * half, c * width))  115 us
  transfers between devices with their start and end apart: 33, of which 15 were waited for; matrix products, arithmetic and copies ran while one was open for 44% of the time, Pallas kernels for 1%

profile of v3, /device:TPU:0, one launch (start us, length us, event | category | flops | bytes accessed | tf_op | source)
XLA Modules:
  0.0 2199.5 jit_solution(11018370763657485509)
XLA Ops:
  57.4 127.3 %collective-permute-done.9 = bf16[1024,4096]{1,0:T(8,128)(2,1)} collective-permute-done((bf16[1024,4096]{1,0:T(8,128)(2,1)}, bf16[1024,4096]{1,0:T(8,128)(2,1)}, u32[]{:S(2)}, u32[]{:S(2)}) %collective-permute-start.9) | collective-permute-done | bytes 8388640 | tf_op jit(solution)/shard_map/ppermute | solution.py:63
  242.8 123.9 %collective-permute-done.2 = bf16[4096,1024]{1,0:T(8,128)(2,1)} collective-permute-done((bf16[4096,1024]{1,0:T(8,128)(2,1)}, bf16[4096,1024]{1,0:T(8,128)(2,1)}, u32[]{:S(2)}, u32[]{:S(2)}) %collective-permute-start.2) | collective-permute-done | bytes 8388640 | tf_op jit(solution)/shard_map/ppermute | solution.py:66
  375.9 23.7 %fusion.56 = f32[2048,1024]{1,0:T(8,128)} fusion(bf16[2048,4096]{1,0:T(8,128)(2,1)S(1)} %pad_maximum_fusion.3, bf16[4096,7168]{1,0:T(8,128)(2,1)} %param.4, s32[]{:T(128)S(6)} %select_n.62), kind=kOutput, calls=%fused_computation.73 | convolution fusion | flops 17179869184 | bytes 33554436 | tf_op jit(solution)/shard_map/dot_general | solution.py:78
  429.9 116.6 %collective-permute-done.5 = bf16[4096,1024]{1,0:T(8,128)(2,1)} collective-permute-done((bf16[4096,1024]{1,0:T(8,128)(2,1)}, bf16[4096,1024]{1,0:T(8,128)(2,1)}, u32[]{:S(2)}, u32[]{:S(2)}) %collective-permute-start.5) | collective-permute-done | bytes 8388640 | tf_op jit(solution)/shard_map/ppermute | solution.py:66
  549.3 25.1 %fusion.23 = bf16[2048,1024]{1,0:T(8,128)(2,1)S(1)} fusion(f32[2048,1024]{1,0:T(8,128)} %fusion.50, bf16[2048,4096]{1,0:T(8,128)(2,1)S(1)} %pad_maximum_fusion, bf16[4096,1024]{1,0:T(8,128)(2,1)} %collective-permute-done.5), kind=kOutput, calls=%fused_computation.39 | convolution fusion | flops 17202937856 | bytes 37748736 | tf_op jit(solution)/shard_map/dot_general | solution.py:78
  574.4 24.0 %fusion.52 = f32[2048,1024]{1,0:T(8,128)} fusion(bf16[2048,4096]{1,0:T(8,128)(2,1)} %copy-done, bf16[4096,7168]{1,0:T(8,128)(2,1)} %param.4, s32[]{:T(128)S(6)} %select_n.66), kind=kOutput, calls=%fused_computation.69 | convolution fusion | flops 17179869184 | bytes 33554436 | tf_op jit(solution)/shard_map/dot_general | solution.py:78
  598.4 25.9 %fusion.15 = bf16[2048,1024]{1,0:T(8,128)(2,1)} fusion(f32[2048,1024]{1,0:T(8,128)} %fusion.54, bf16[2048,4096]{1,0:T(8,128)(2,1)S(1)} %pad_maximum_fusion, bf16[4096,1024]{1,0:T(8,128)(2,1)} %collective-permute-done.2), kind=kOutput, calls=%fused_computation.31 | convolution fusion | flops 17202937856 | bytes 37748736 | tf_op jit(solution)/shard_map/dot_general | solution.py:78
  624.3 102.0 %collective-permute-done.3 = bf16[4096,1024]{1,0:T(8,128)(2,1)} collective-permute-done((bf16[4096,1024]{1,0:T(8,128)(2,1)}, bf16[4096,1024]{1,0:T(8,128)(2,1)}, u32[]{:S(2)}, u32[]{:S(2)}) %collective-permute-start.3) | collective-permute-done | bytes 8388640 | tf_op jit(solution)/shard_map/ppermute | solution.py:66
  726.3 25.7 %fusion.7 = bf16[2048,1024]{1,0:T(8,128)(2,1)} fusion(f32[2048,1024]{1,0:T(8,128)} %fusion.58, bf16[2048,4096]{1,0:T(8,128)(2,1)S(1)} %pad_maximum_fusion, bf16[4096,1024]{1,0:T(8,128)(2,1)} %collective-permute-done.3), kind=kOutput, calls=%fused_computation.23 | convolution fusion | flops 17202937856 | bytes 37748736 | tf_op jit(solution)/shard_map/dot_general | solution.py:78
  780.7 34.8 %collective-permute-done.6 = bf16[4096,512]{1,0:T(8,128)(2,1)} collective-permute-done((bf16[4096,512]{1,0:T(8,128)(2,1)}, bf16[4096,512]{1,0:T(8,128)(2,1)}, u32[]{:S(2)}, u32[]{:S(2)}) %collective-permute-start.6) | collective-permute-done | bytes 4194336 | tf_op jit(solution)/shard_map/ppermute | solution.py:66
  847.6 23.5 %fusion.102 = f32[2048,1024]{1,0:T(8,128)} fusion(bf16[2048,4096]{1,0:T(8,128)(2,1)S(1)} %pad_maximum_fusion.2, bf16[4096,1024]{1,0:T(8,128)(2,1)} %collective-permute-done.2), kind=kOutput, calls=%fused_computation.173 | convolution fusion | flops 17179869184 | bytes 33554432 | tf_op jit(solution)/shard_map/dot_general | solution.py:78
  879.4 23.1 %fusion.103 = f32[2048,1024]{1,0:T(8,128)} fusion(bf16[2048,4096]{1,0:T(8,128)(2,1)S(1)} %pad_maximum_fusion.2, bf16[4096,1024]{1,0:T(8,128)(2,1)} %collective-permute-done.5), kind=kOutput, calls=%fused_computation.174 | convolution fusion | flops 17179869184 | bytes 33554432 | tf_op jit(solution)/shard_map/dot_general | solution.py:78
  923.9 23.1 %fusion.104 = f32[2048,1024]{1,0:T(8,128)} fusion(bf16[2048,4096]{1,0:T(8,128)(2,1)S(1)} %pad_maximum_fusion.2, bf16[4096,1024]{1,0:T(8,128)(2,1)} %collective-permute-done.3), kind=kOutput, calls=%fused_computation.175 | convolution fusion | flops 17179869184 | bytes 33554432 | tf_op jit(solution)/shard_map/dot_general | solution.py:78
  1014.5 22.7 %dynamic_update_slice.34 = bf16[7168,4096]{1,0:T(8,128)(2,1)} pad(bf16[3584,2048]{1,0:T(8,128)(2,1)} %get-tuple-element.31, bf16[]{:T(256)} %constant.48.clone.1), padding=0_3584x0_2048 | pad | bytes 73400320 | tf_op jit(solution)/shard_map/dynamic_update_slice | solution.py:131
  1037.2 25.2 %dynamic_update_slice.30 = bf16[7168,4096]{1,0:T(8,128)(2,1)} pad(bf16[3584,2048]{1,0:T(8,128)(2,1)} %get-tuple-element.32, bf16[]{:T(256)} %constant.48.clone.1), padding=0_3584x0_2048 | pad | bytes 73400320 | tf_op jit(solution)/shard_map/dynamic_update_slice | solution.py:131
  1076.6 51.4 %collective-permute-done.25 = bf16[512,3072]{1,0:T(8,128)(2,1)} collective-permute-done((bf16[512,3072]{1,0:T(8,128)(2,1)}, bf16[512,3072]{1,0:T(8,128)(2,1)}, u32[]{:S(2)}, u32[]{:S(2)}) %collective-permute-start.25) | collective-permute-done | bytes 3145760 | tf_op jit(solution)/shard_map/ppermute | solution.py:66
  1152.0 133.2 %collective-permute-done.20 = bf16[512,3584]{1,0:T(8,128)(2,1)S(1)} collective-permute-done((bf16[512,3584]{1,0:T(8,128)(2,1)S(1)}, bf16[512,3584]{1,0:T(8,128)(2,1)S(1)}, u32[]{:S(2)}, u32[]{:S(2)}) %collective-permute-start.20) | collective-permute-done | bytes 3670048 | tf_op jit(solution)/shard_map/ppermute | solution.py:66
  1294.7 69.2 %collective-permute-done.13 = bf16[512,3584]{1,0:T(8,128)(2,1)} collective-permute-done((bf16[512,3584]{1,0:T(8,128)(2,1)}, bf16[512,3584]{1,0:T(8,128)(2,1)}, u32[]{:S(2)}, u32[]{:S(2)}) %collective-permute-start.13) | collective-permute-done | bytes 3670048 | tf_op jit(solution)/shard_map/ppermute | solution.py:66
  1364.0 78.5 %collective-permute-done.14 = bf16[512,3584]{1,0:T(8,128)(2,1)} collective-permute-done((bf16[512,3584]{1,0:T(8,128)(2,1)}, bf16[512,3584]{1,0:T(8,128)(2,1)}, u32[]{:S(2)}, u32[]{:S(2)}) %collective-permute-start.14) | collective-permute-done | bytes 3670048 | tf_op jit(solution)/shard_map/ppermute | solution.py:69
  1451.4 30.5 %collective-permute-done.30 = bf16[256,3584]{1,0:T(8,128)(2,1)} collective-permute-done((bf16[256,3584]{1,0:T(8,128)(2,1)}, bf16[256,3584]{1,0:T(8,128)(2,1)}, u32[]{:S(2)}, u32[]{:S(2)}) %collective-permute-start.30) | collective-permute-done | bytes 1835040 | tf_op jit(solution)/shard_map/ppermute | solution.py:66
  1483.0 38.1 %collective-permute-done.31 = bf16[256,3584]{1,0:T(8,128)(2,1)} collective-permute-done((bf16[256,3584]{1,0:T(8,128)(2,1)}, bf16[256,3584]{1,0:T(8,128)(2,1)}, u32[]{:S(2)}, u32[]{:S(2)}) %collective-permute-start.31) | collective-permute-done | bytes 1835040 | tf_op jit(solution)/shard_map/ppermute | solution.py:69
  1592.1 25.9 %fusion.109 = f32[256,4096]{1,0:T(8,128)} fusion(bf16[256,7168]{1,0:T(8,128)(2,1)} %constant_dynamic-update-slice_fusion.21, bf16[7168,4096]{1,0:T(8,128)(2,1)} %get-tuple-element.25), kind=kOutput, calls=%fused_computation.180 | convolution fusion | flops 15032385536 | bytes 66584576 | tf_op jit(solution)/shard_map/dot_general | solution.py:78
  1618.0 39.7 %fusion.108 = f32[512,4096]{1,0:T(8,128)} fusion(bf16[512,7168]{1,0:T(8,128)(2,1)} %constant_dynamic-update-slice_fusion.15, bf16[7168,4096]{1,0:T(8,128)(2,1)} %get-tuple-element.25), kind=kOutput, calls=%fused_computation.179 | convolution fusion | flops 30064771072 | bytes 74448896 | tf_op jit(solution)/shard_map/dot_general | solution.py:78
  1657.7 39.9 %fusion.107 = f32[512,4096]{1,0:T(8,128)} fusion(bf16[512,7168]{1,0:T(8,128)(2,1)} %copy-done.30, bf16[7168,4096]{1,0:T(8,128)(2,1)} %get-tuple-element.25), kind=kOutput, calls=%fused_computation.178 | convolution fusion | flops 30064771072 | bytes 74448896 | tf_op jit(solution)/shard_map/dot_general | solution.py:78
  1697.6 37.9 %fusion.105 = f32[512,4096]{1,0:T(8,128)} fusion(bf16[512,7168]{1,0:T(8,128)(2,1)S(1)} %bitcast.54, bf16[7168,4096]{1,0:T(8,128)(2,1)} %get-tuple-element.25), kind=kOutput, calls=%fused_computation.176 | convolution fusion | flops 30064771072 | bytes 74448896 | tf_op jit(solution)/shard_map/dot_general | solution.py:78
  1735.5 40.4 %convolution_add_fusion.1 = f32[512,4096]{1,0:T(8,128)} fusion(f32[512,4096]{1,0:T(8,128)} %fusion.105, bf16[512,7168]{1,0:T(8,128)(2,1)} %pad_maximum_fusion.4, bf16[7168,4096]{1,0:T(8,128)(2,1)} %get-tuple-element.26.refs_0_.refs_1_.refs_2_.refs_3_), kind=kOutput, calls=%fused_computation.83 | convolution fusion | flops 30066868224 | bytes 82837504 | tf_op jit(solution)/shard_map/dot_general | solution.py:78
  1776.1 40.4 %convolution_add_fusion = f32[512,4096]{1,0:T(8,128)} fusion(f32[512,4096]{1,0:T(8,128)} %fusion.108, bf16[512,7168]{1,0:T(8,128)(2,1)} %pad_maximum_fusion.6, bf16[7168,4096]{1,0:T(8,128)(2,1)} %get-tuple-element.26.refs_0_.refs_1_.refs_2_.refs_3_), kind=kOutput, calls=%fused_computation.82 | convolution fusion | flops 30066868224 | bytes 82837504 | tf_op jit(solution)/shard_map/dot_general | solution.py:78
  1816.4 26.2 %fusion.101.refs_1_ = f32[256,4096]{1,0:T(8,128)} fusion(bf16[256,7168]{1,0:T(8,128)(2,1)} %constant_dynamic-update-slice_fusion, bf16[7168,4096]{1,0:T(8,128)(2,1)} %get-tuple-element.25), kind=kOutput, calls=%fused_computation.172 | convolution fusion | flops 15032385536 | bytes 66584576 | tf_op jit(solution)/shard_map/dot_general | solution.py:78
  1844.5 39.5 %fusion.106 = f32[512,4096]{1,0:T(8,128)} fusion(bf16[512,7168]{1,0:T(8,128)(2,1)} %pad_maximum_fusion.5, bf16[7168,4096]{1,0:T(8,128)(2,1)} %get-tuple-element.26.refs_0_.refs_1_.refs_2_.refs_3_), kind=kOutput, calls=%fused_computation.177 | convolution fusion | flops 30064771072 | bytes 74448896 | tf_op jit(solution)/shard_map/dot_general | solution.py:78
  1884.0 75.6 %collective-permute-done.23.refs_2_ = f32[512,4096]{1,0:T(8,128)} collective-permute-done((f32[512,4096]{1,0:T(8,128)}, f32[512,4096]{1,0:T(8,128)}, u32[]{:S(2)}, u32[]{:S(2)}) %collective-permute-start.23) | collective-permute-done | bytes 8388640 | tf_op jit(solution)/shard_map/ppermute | solution.py:63
  1959.6 27.0 %fusion.61 = bf16[256,4096]{1,0:T(8,128)(2,1)} fusion(f32[256,4096]{1,0:T(8,128)} %fusion.109, bf16[256,7168]{1,0:T(8,128)(2,1)} %pad_maximum_fusion.11, bf16[7168,4096]{1,0:T(8,128)(2,1)} %get-tuple-element.26.refs_0_.refs_1_.refs_2_.refs_3_, f32[512,4096]{1,0:T(8,128)} %collective-permute-done.23.refs_2_), kind=kOutput, calls=%fused_computation.86 | convolution fusion | flops 15035531264 | bytes 72876032 | tf_op jit(solution)/shard_map/dot_general | solution.py:78
  1986.6 151.9 %collective-permute-done.29 = f32[512,4096]{1,0:T(8,128)} collective-permute-done((f32[512,4096]{1,0:T(8,128)}, f32[512,4096]{1,0:T(8,128)}, u32[]{:S(2)}, u32[]{:S(2)}) %collective-permute-start.29) | collective-permute-done | bytes 8388640 | tf_op jit(solution)/shard_map/ppermute | solution.py:63
  (214 shorter events, 506.8 us)
Async XLA Ops:
  0.0 26.9 %collective-permute-start.4 = (bf16[1024,4096]{1,0:T(8,128)(2,1)}, bf16[1024,4096]{1,0:T(8,128)(2,1)}, u32[]{:S(2)}, u32[]{:S(2)}) collective-permute-start(bf16[1024,4096]{1,0:T(8,128)(2,1)} %param.3), channel_id=1, source_target_pairs={{0,1},{1,0},{2,3},{3,2},{4,5},{5,4},{6,7},{7,6}} | collective-permute-start | bytes 25165832 | tf_op jit(solution)/shard_map/ppermute | solution.py:60
  0.8 183.9 %collective-permute-start.9 = (bf16[1024,4096]{1,0:T(8,128)(2,1)}, bf16[1024,4096]{1,0:T(8,128)(2,1)}, u32[]{:S(2)}, u32[]{:S(2)}) collective-permute-start(bf16[1024,4096]{1,0:T(8,128)(2,1)} %param.3), channel_id=1, source_target_pairs={{0,4},{4,0},{1,5},{5,1},{2,6},{6,2},{3,7},{7,3}} | collective-permute-start | bytes 25165832 | tf_op jit(solution)/shard_map/ppermute | solution.py:63
  3.3 237.8 %collective-permute-start = (bf16[1024,4096]{1,0:T(8,128)(2,1)}, bf16[1024,4096]{1,0:T(8,128)(2,1)}, u32[]{:S(2)}, u32[]{:S(2)}) collective-permute-start(bf16[1024,4096]{1,0:T(8,128)(2,1)} %param.3), channel_id=1, source_target_pairs={{0,2},{2,0},{1,3},{3,1},{4,6},{6,4},{5,7},{7,5}} | collective-permute-start | bytes 25165832 | tf_op jit(solution)/shard_map/ppermute | solution.py:66
  21.7 345.0 %collective-permute-start.2 = (bf16[4096,1024]{1,0:T(8,128)(2,1)}, bf16[4096,1024]{1,0:T(8,128)(2,1)}, u32[]{:S(2)}, u32[]{:S(2)}) collective-permute-start(bf16[4096,1024]{1,0:T(8,128)(2,1)} %get-tuple-element.33), channel_id=1, source_target_pairs={{0,2},{2,0},{1,3},{3,1},{4,6},{6,4},{5,7},{7,5}} | collective-permute-start | bytes 25165832 | tf_op jit(solution)/shard_map/ppermute | solution.py:66
  22.3 1503.1 %collective-permute-start.16 = (bf16[14336,2048]{1,0:T(8,128)(2,1)}, bf16[14336,2048]{1,0:T(8,128)(2,1)}, u32[]{:S(2)}, u32[]{:S(2)}) collective-permute-start(bf16[14336,2048]{1,0:T(8,128)(2,1)} %param.5), channel_id=1, source_target_pairs={{0,1},{1,0},{2,3},{3,2},{4,5},{5,4},{6,7},{7,6}} | collective-permute-start | bytes 176160768 | tf_op jit(solution)/shard_map/ppermute | solution.py:60
  184.8 184.0 %collective-permute-start.10 = (bf16[1024,4096]{1,0:T(8,128)(2,1)}, bf16[1024,4096]{1,0:T(8,128)(2,1)S(1)}, u32[]{:S(2)}, u32[]{:S(2)}) collective-permute-start(bf16[1024,4096]{1,0:T(8,128)(2,1)} %collective-permute-done.9), channel_id=1, source_target_pairs={{0,1},{1,0},{2,3},{3,2},{4,5},{5,4},{6,7},{7,6}} | collective-permute-start | bytes 25165832 | tf_op jit(solution)/shard_map/ppermute | solution.py:60
  241.1 305.4 %collective-permute-start.5 = (bf16[4096,1024]{1,0:T(8,128)(2,1)}, bf16[4096,1024]{1,0:T(8,128)(2,1)}, u32[]{:S(2)}, u32[]{:S(2)}) collective-permute-start(bf16[4096,1024]{1,0:T(8,128)(2,1)} %get-tuple-element.16), channel_id=1, source_target_pairs={{0,2},{2,0},{1,3},{3,1},{4,6},{6,4},{5,7},{7,5}} | collective-permute-start | bytes 25165832 | tf_op jit(solution)/shard_map/ppermute | solution.py:66
  366.8 359.5 %collective-permute-start.3 = (bf16[4096,1024]{1,0:T(8,128)(2,1)}, bf16[4096,1024]{1,0:T(8,128)(2,1)}, u32[]{:S(2)}, u32[]{:S(2)}) collective-permute-start(bf16[4096,1024]{1,0:T(8,128)(2,1)} %get-tuple-element.15), channel_id=1, source_target_pairs={{0,2},{2,0},{1,3},{3,1},{4,6},{6,4},{5,7},{7,5}} | collective-permute-start | bytes 25165832 | tf_op jit(solution)/shard_map/ppermute | solution.py:66
  368.2 181.0 %collective-permute-start.7 = (bf16[1024,4096]{1,0:T(8,128)(2,1)}, bf16[1024,4096]{1,0:T(8,128)(2,1)}, u32[]{:S(2)}, u32[]{:S(2)}) collective-permute-start(bf16[1024,4096]{1,0:T(8,128)(2,1)} %collective-permute-done), channel_id=1, source_target_pairs={{0,4},{4,0},{1,5},{5,1},{2,6},{6,2},{3,7},{7,3}} | collective-permute-start | bytes 25165832 | tf_op jit(solution)/shard_map/ppermute | solution.py:63
  368.8 52.8 %collective-permute-start.1 = (bf16[1024,4096]{1,0:T(8,128)(2,1)}, bf16[1024,4096]{1,0:T(8,128)(2,1)}, u32[]{:S(2)}, u32[]{:S(2)}) collective-permute-start(bf16[1024,4096]{1,0:T(8,128)(2,1)} %collective-permute-done), channel_id=1, source_target_pairs={{0,1},{1,0},{2,3},{3,2},{4,5},{5,4},{6,7},{7,6}} | collective-permute-start | bytes 25165832 | tf_op jit(solution)/shard_map/ppermute | solution.py:60
  546.5 268.9 %collective-permute-start.6 = (bf16[4096,512]{1,0:T(8,128)(2,1)}, bf16[4096,512]{1,0:T(8,128)(2,1)}, u32[]{:S(2)}, u32[]{:S(2)}) collective-permute-start(bf16[4096,512]{1,0:T(8,128)(2,1)} %constant_dynamic-slice_fusion.3), channel_id=1, source_target_pairs={{0,2},{2,0},{1,3},{3,1},{4,6},{6,4},{5,7},{7,5}} | collective-permute-start | bytes 12582920 | tf_op jit(solution)/shard_map/ppermute | solution.py:66
  549.3 289.4 %collective-permute-start.8 = (bf16[1024,4096]{1,0:T(8,128)(2,1)}, bf16[1024,4096]{1,0:T(8,128)(2,1)}, u32[]{:S(2)}, u32[]{:S(2)}) collective-permute-start(bf16[1024,4096]{1,0:T(8,128)(2,1)} %collective-permute-done.7), channel_id=1, source_target_pairs={{0,1},{1,0},{2,3},{3,2},{4,5},{5,4},{6,7},{7,6}} | collective-permute-start | bytes 25165832 | tf_op jit(solution)/shard_map/ppermute | solution.py:60
  833.7 130.6 %collective-permute-start.19 = (bf16[256,3584]{1,0:T(8,128)(2,1)}, bf16[256,3584]{1,0:T(8,128)(2,1)}, u32[]{:S(2)}, u32[]{:S(2)}) collective-permute-start(bf16[256,3584]{1,0:T(8,128)(2,1)} %pad_maximum_fusion.14), channel_id=1, source_target_pairs={{0,1},{1,0},{2,3},{3,2},{4,5},{5,4},{6,7},{7,6}} | collective-permute-start | bytes 5505032 | tf_op jit(solution)/shard_map/ppermute | solution.py:60
  835.0 130.4 %collective-permute-start.32 = (bf16[256,3584]{1,0:T(8,128)(2,1)}, bf16[256,3584]{1,0:T(8,128)(2,1)}, u32[]{:S(2)}, u32[]{:S(2)}) collective-permute-start(bf16[256,3584]{1,0:T(8,128)(2,1)} %pad_maximum_fusion.16), channel_id=1, source_target_pairs={{0,1},{1,0},{2,3},{3,2},{4,5},{5,4},{6,7},{7,6}} | collective-permute-start | bytes 5505032 | tf_op jit(solution)/shard_map/ppermute | solution.py:60
  838.7 129.3 %collective-permute-start.24 = (bf16[512,3584]{1,0:T(8,128)(2,1)}, bf16[512,3584]{1,0:T(8,128)(2,1)}, u32[]{:S(2)}, u32[]{:S(2)}) collective-permute-start(bf16[512,3584]{1,0:T(8,128)(2,1)} %pad_maximum_fusion.8), channel_id=1, source_target_pairs={{0,1},{1,0},{2,3},{3,2},{4,5},{5,4},{6,7},{7,6}} | collective-permute-start | bytes 11010056 | tf_op jit(solution)/shard_map/ppermute | solution.py:60
  960.2 30.6 %collective-permute-start.28 = (bf16[512,512]{1,0:T(8,128)(2,1)S(1)}, bf16[512,512]{1,0:T(8,128)(2,1)S(1)}, u32[]{:S(2)}, u32[]{:S(2)}) collective-permute-start(bf16[512,512]{1,0:T(8,128)(2,1)S(1)} %get-tuple-element.98), channel_id=1, source_target_pairs={{0,1},{1,0},{2,3},{3,2},{4,5},{5,4},{6,7},{7,6}} | collective-permute-start | bytes 1572872 | tf_op jit(solution)/shard_map/ppermute | solution.py:60
  964.3 27.1 %collective-permute-start.12 = (bf16[512,512]{1,0:T(8,128)(2,1)S(1)}, bf16[512,512]{1,0:T(8,128)(2,1)}, u32[]{:S(2)}, u32[]{:S(2)}) collective-permute-start(bf16[512,512]{1,0:T(8,128)(2,1)S(1)} %get-tuple-element.98), channel_id=1, source_target_pairs={{0,3},{1,2},{2,1},{3,0},{4,7},{5,6},{6,5},{7,4}} | collective-permute-start | bytes 1572872 | tf_op jit(solution)/shard_map/ppermute | solution.py:69
  968.0 102.9 %collective-permute-start.27 = (bf16[512,3072]{1,0:T(8,128)(2,1)}, bf16[512,3072]{1,0:T(8,128)(2,1)}, u32[]{:S(2)}, u32[]{:S(2)}) collective-permute-start(bf16[512,3072]{1,0:T(8,128)(2,1)} %pad_maximum_fusion.13), channel_id=1, source_target_pairs={{0,1},{1,0},{2,3},{3,2},{4,5},{5,4},{6,7},{7,6}} | collective-permute-start | bytes 9437192 | tf_op jit(solution)/shard_map/ppermute | solution.py:60
  989.8 81.9 %collective-permute-start.26 = (bf16[512,3072]{1,0:T(8,128)(2,1)}, bf16[512,3072]{1,0:T(8,128)(2,1)}, u32[]{:S(2)}, u32[]{:S(2)}) collective-permute-start(bf16[512,3072]{1,0:T(8,128)(2,1)} %pad_maximum_fusion.13), channel_id=1, source_target_pairs={{0,3},{1,2},{2,1},{3,0},{4,7},{5,6},{6,5},{7,4}} | collective-permute-start | bytes 9437192 | tf_op jit(solution)/shard_map/ppermute | solution.py:69
  990.9 137.2 %collective-permute-start.25 = (bf16[512,3072]{1,0:T(8,128)(2,1)}, bf16[512,3072]{1,0:T(8,128)(2,1)}, u32[]{:S(2)}, u32[]{:S(2)}) collective-permute-start(bf16[512,3072]{1,0:T(8,128)(2,1)} %pad_maximum_fusion.12), channel_id=1, source_target_pairs={{0,2},{2,0},{1,3},{3,1},{4,6},{6,4},{5,7},{7,5}} | collective-permute-start | bytes 9437192 | tf_op jit(solution)/shard_map/ppermute | solution.py:66
  991.6 137.9 %collective-permute-start.22 = (bf16[512,3584]{1,0:T(8,128)(2,1)}, bf16[512,3584]{1,0:T(8,128)(2,1)}, u32[]{:S(2)}, u32[]{:S(2)}) collective-permute-start(bf16[512,3584]{1,0:T(8,128)(2,1)} %pad_maximum_fusion.10), channel_id=1, source_target_pairs={{0,1},{1,0},{2,3},{3,2},{4,5},{5,4},{6,7},{7,6}} | collective-permute-start | bytes 11010056 | tf_op jit(solution)/shard_map/ppermute | solution.py:60
  1070.9 214.3 %collective-permute-start.21 = (bf16[512,3584]{1,0:T(8,128)(2,1)}, bf16[512,3584]{1,0:T(8,128)(2,1)S(1)}, u32[]{:S(2)}, u32[]{:S(2)}) collective-permute-start(bf16[512,3584]{1,0:T(8,128)(2,1)} %pad_maximum_fusion.10), channel_id=1, source_target_pairs={{0,3},{1,2},{2,1},{3,0},{4,7},{5,6},{6,5},{7,4}} | collective-permute-start | bytes 11010056 | tf_op jit(solution)/shard_map/ppermute | solution.py:69
  1071.7 213.5 %collective-permute-start.20 = (bf16[512,3584]{1,0:T(8,128)(2,1)S(1)}, bf16[512,3584]{1,0:T(8,128)(2,1)S(1)}, u32[]{:S(2)}, u32[]{:S(2)}) collective-permute-start(bf16[512,3584]{1,0:T(8,128)(2,1)S(1)} %pad_maximum_fusion.9), channel_id=1, source_target_pairs={{0,2},{2,0},{1,3},{3,1},{4,6},{6,4},{5,7},{7,5}} | collective-permute-start | bytes 11010056 | tf_op jit(solution)/shard_map/ppermute | solution.py:66
  1128.0 235.9 %collective-permute-start.13 = (bf16[512,3584]{1,0:T(8,128)(2,1)}, bf16[512,3584]{1,0:T(8,128)(2,1)}, u32[]{:S(2)}, u32[]{:S(2)}) collective-permute-start(bf16[512,3584]{1,0:T(8,128)(2,1)} %pad_maximum_fusion.7), channel_id=1, source_target_pairs={{0,2},{2,0},{1,3},{3,1},{4,6},{6,4},{5,7},{7,5}} | collective-permute-start | bytes 11010056 | tf_op jit(solution)/shard_map/ppermute | solution.py:66
  1129.5 312.9 %collective-permute-start.14 = (bf16[512,3584]{1,0:T(8,128)(2,1)}, bf16[512,3584]{1,0:T(8,128)(2,1)}, u32[]{:S(2)}, u32[]{:S(2)}) collective-permute-start(bf16[512,3584]{1,0:T(8,128)(2,1)} %pad_maximum_fusion.8), channel_id=1, source_target_pairs={{0,3},{1,2},{2,1},{3,0},{4,7},{5,6},{6,5},{7,4}} | collective-permute-start | bytes 11010056 | tf_op jit(solution)/shard_map/ppermute | solution.py:69
  1287.2 194.8 %collective-permute-start.30 = (bf16[256,3584]{1,0:T(8,128)(2,1)}, bf16[256,3584]{1,0:T(8,128)(2,1)}, u32[]{:S(2)}, u32[]{:S(2)}) collective-permute-start(bf16[256,3584]{1,0:T(8,128)(2,1)} %pad_maximum_fusion.15), channel_id=1, source_target_pairs={{0,2},{2,0},{1,3},{3,1},{4,6},{6,4},{5,7},{7,5}} | collective-permute-start | bytes 5505032 | tf_op jit(solution)/shard_map/ppermute | solution.py:66
  1288.7 232.5 %collective-permute-start.31 = (bf16[256,3584]{1,0:T(8,128)(2,1)}, bf16[256,3584]{1,0:T(8,128)(2,1)}, u32[]{:S(2)}, u32[]{:S(2)}) collective-permute-start(bf16[256,3584]{1,0:T(8,128)(2,1)} %pad_maximum_fusion.16), channel_id=1, source_target_pairs={{0,3},{1,2},{2,1},{3,0},{4,7},{5,6},{6,5},{7,4}} | collective-permute-start | bytes 5505032 | tf_op jit(solution)/shard_map/ppermute | solution.py:69
  1442.5 745.8 %collective-permute-start.15 = (bf16[256,1536]{1,0:T(8,128)(2,1)}, bf16[256,1536]{1,0:T(8,128)(2,1)}, u32[]{:S(2)}, u32[]{:S(2)}) collective-permute-start(bf16[256,1536]{1,0:T(8,128)(2,1)} %pad_maximum_fusion.18), channel_id=1, source_target_pairs={{0,2},{2,0},{1,3},{3,1},{4,6},{6,4},{5,7},{7,5}} | collective-permute-start | bytes 2359304 | tf_op jit(solution)/shard_map/ppermute | solution.py:66
  1444.0 727.5 %collective-permute-start.17 = (bf16[256,2048]{1,0:T(8,128)(2,1)}, bf16[256,2048]{1,0:T(8,128)(2,1)}, u32[]{:S(2)}, u32[]{:S(2)}) collective-permute-start(bf16[256,2048]{1,0:T(8,128)(2,1)} %pad_maximum_fusion.17), channel_id=1, source_target_pairs={{0,2},{2,0},{1,3},{3,1},{4,6},{6,4},{5,7},{7,5}} | collective-permute-start | bytes 3145736 | tf_op jit(solution)/shard_map/ppermute | solution.py:66
  1482.0 671.5 %collective-permute-start.18 = (bf16[256,3584]{1,0:T(8,128)(2,1)}, bf16[256,3584]{1,0:T(8,128)(2,1)}, u32[]{:S(2)}, u32[]{:S(2)}) collective-permute-start(bf16[256,3584]{1,0:T(8,128)(2,1)} %pad_maximum_fusion.14), channel_id=1, source_target_pairs={{0,3},{1,2},{2,1},{3,0},{4,7},{5,6},{6,5},{7,4}} | collective-permute-start | bytes 5505032 | tf_op jit(solution)/shard_map/ppermute | solution.py:69
  1775.9 183.6 %collective-permute-start.23 = (f32[512,4096]{1,0:T(8,128)}, f32[512,4096]{1,0:T(8,128)}, u32[]{:S(2)}, u32[]{:S(2)}) collective-permute-start(f32[512,4096]{1,0:T(8,128)} %convolution_add_fusion.1), channel_id=1, source_target_pairs={{0,4},{4,0},{1,5},{5,1},{2,6},{6,2},{3,7},{7,3}} | collective-permute-start | bytes 25165832 | tf_op jit(solution)/shard_map/ppermute | solution.py:63
  1842.6 295.9 %collective-permute-start.29 = (f32[512,4096]{1,0:T(8,128)}, f32[512,4096]{1,0:T(8,128)}, u32[]{:S(2)}, u32[]{:S(2)}) collective-permute-start(f32[512,4096]{1,0:T(8,128)} %convolution_add_fusion), channel_id=1, source_target_pairs={{0,4},{4,0},{1,5},{5,1},{2,6},{6,2},{3,7},{7,3}} | collective-permute-start | bytes 25165832 | tf_op jit(solution)/shard_map/ppermute | solution.py:63
  (46 other events, 1658.4 us)
